TPU v7x, 16 devices: a 4x2x1 block of a 4x4x8 slice. The times are simulated.
16 devices in a mesh: replica: 2 (over y, z), model: 8 (over x, core).
Axes of the slice: x: 4, y: 2, z: 1, core: 2. Of those that a mesh axis runs over, the one named last changes fastest.
The devices are a block of a 4x4x8 slice.
Arguments:
- x: bfloat16 [256, 16384], P('replica'), parts along dimension 0
- w_query: bfloat16 [16384, 16384], P(None, 'model')
- w_key: bfloat16 [16384, 1024], replicated
- w_value: bfloat16 [16384, 1024], replicated
- w_out: bfloat16 [16384, 16384], P('model')
- k_cache: bfloat16 [256, 8, 256, 128], P('replica'), parts along dimension 0
- v_cache: bfloat16 [256, 8, 256, 128], P('replica'), parts along dimension 0
- lengths: int32 [256], P('replica'), parts along dimension 0
Outputs:
- output 1: bfloat16 [256, 16384], P('replica'), parts along dimension 0
- output 2: bfloat16 [256, 8, 128], P('replica'), parts along dimension 0
- output 3: bfloat16 [256, 8, 128], P('replica'), parts along dimension 0
There are 2 independent parts. A program takes and returns all parts, laid end to end along the dimension named above; an argument that names none is the same for every part.
All inputs are finite; a program needn't handle non-finite values.
Results may differ from a plain program's by a relative error of at most 0.00333699.
Values are sent between devices in bfloat16 or wider.
A program may use at most 768 MiB of HBM per device.

v0:
```python
import jax
import jax.numpy as jnp
from jax import lax
from jax.sharding import PartitionSpec as P


def attend(queries, k_rows, v_rows, k_one, v_one, seq_lens):
    inv_sqrt = queries.shape[-1] ** -0.5
    scores = jnp.einsum("bgrd,bgtd->bgrt", queries, k_rows, preferred_element_type=jnp.float32) * inv_sqrt
    score_new = jnp.einsum("bgrd,bgd->bgr", queries, k_one, preferred_element_type=jnp.float32) * inv_sqrt
    positions = jnp.arange(k_rows.shape[2])
    in_range = positions[None, None, None, :] < seq_lens[:, None, None, None]
    scores = jnp.where(in_range, scores, -jnp.inf)
    row_max = jnp.maximum(jnp.max(scores, axis=-1), score_new)
    weights = jnp.exp(scores - row_max[..., None])
    weight_new = jnp.exp(score_new - row_max)
    norm_sum = jnp.sum(weights, axis=-1) + weight_new
    out_sum = jnp.einsum("bgrt,bgtd->bgrd", weights.astype(jnp.bfloat16), v_rows, preferred_element_type=jnp.float32)
    out_sum = out_sum + weight_new.astype(jnp.bfloat16).astype(jnp.float32)[..., None] * v_one.astype(jnp.float32)[:, :, None, :]
    return (out_sum / norm_sum[..., None]).astype(jnp.bfloat16)


def solution(mesh):
    model_size = mesh.shape["model"]

    def local_step(x, w_query, w_key, w_value, w_out, k_cache, v_cache, lengths):
        batch_rows = x.shape[0]
        kv_heads = k_cache.shape[1]
        head_dim = k_cache.shape[3]
        local_rows = batch_rows // model_size
        row_start = lax.axis_index("model") * local_rows
        q_local = jnp.dot(x, w_query, preferred_element_type=jnp.float32).astype(jnp.bfloat16)
        q_rows = lax.all_to_all(q_local, "model", 0, 1, tiled=True)
        k_new = jnp.dot(x, w_key, preferred_element_type=jnp.float32).astype(jnp.bfloat16).reshape(batch_rows, kv_heads, head_dim)
        v_new = jnp.dot(x, w_value, preferred_element_type=jnp.float32).astype(jnp.bfloat16).reshape(batch_rows, kv_heads, head_dim)
        queries = q_rows.reshape(local_rows, kv_heads, -1, head_dim)
        out_rows = attend(
            queries,
            lax.dynamic_slice_in_dim(k_cache, row_start, local_rows, axis=0),
            lax.dynamic_slice_in_dim(v_cache, row_start, local_rows, axis=0),
            lax.dynamic_slice_in_dim(k_new, row_start, local_rows, axis=0),
            lax.dynamic_slice_in_dim(v_new, row_start, local_rows, axis=0),
            lax.dynamic_slice_in_dim(lengths, row_start, local_rows, axis=0),
        )
        out_heads = lax.all_to_all(out_rows.reshape(local_rows, -1), "model", 1, 0, tiled=True)
        part_sum = jnp.dot(out_heads, w_out, preferred_element_type=jnp.float32)
        full_sum = lax.psum(part_sum, "model")
        y = (x.astype(jnp.float32) + full_sum).astype(jnp.bfloat16)
        return y, k_new, v_new

    rows_spec = P("replica")
    return jax.shard_map(
        local_step,
        mesh=mesh,
        in_specs=(P("replica", None), P(None, "model"), P(), P(), P("model", None), rows_spec, rows_spec, rows_spec),
        out_specs=(rows_spec, rows_spec, rows_spec),
        check_vma=False,
    )
```

profile of v0, /device:TPU:113, one launch (start us, length us, event | category | flops | bytes accessed | tf_op | source)
XLA Modules:
  0.0 231.9 jit_solution(12697582071696113391)
XLA Ops:
  7.2 25.6 %convolution_convert_fusion = bf16[128,2048]{1,0:T(8,128)(2,1)} fusion(bf16[128,16384]{1,0:T(8,128)(2,1)} %param.8, bf16[16384,2048]{1,0:T(8,128)(2,1)} %param.9), kind=kOutput, calls=%fused_computation.5 | convolution fusion | flops 8590196736 | bytes 71827456 | tf_op jit(solution)/shard_map/dot_general | solution.py:32
  32.7 6.0 %all-to-all-start = ((bf16[8,16,2048]{2,1,0:T(8,128)(2,1)}), bf16[8,16,2048]{2,1,0:T(8,128)(2,1)S(1)}, u32[]{:S(2)}, u32[]{:S(2)}) async-start(bf16[8,16,2048]{2,1,0:T(8,128)(2,1)} %bitcast), calls=%async_computation | async-start | bytes 1048576 | tf_op jit(solution)/shard_map/all_to_all | solution.py:33
  38.8 0.0 all-reduce.2.cloned.1.call-start
  38.8 0.0 copy-start
  38.8 16.4 %fusion.10 = bf16[16,8,8,128]{3,1,2,0:T(8,128)(2,1)S(1)} fusion(bf16[128,16384]{1,0:T(8,128)(2,1)} %param.8, bf16[16384,1024]{1,0:T(8,128)(2,1)} %param.10), kind=kOutput, calls=%fused_computation.14 | convolution fusion | flops 4295098368 | bytes 38010880 | tf_op jit(solution)/shard_map/dot_general | solution.py:34
  55.2 0.0 copy-done
  55.2 0.0 copy-start.3
  55.2 13.0 %fusion.11 = bf16[16,8,8,128]{3,1,2,0:T(8,128)(2,1)S(1)} fusion(bf16[128,16384]{1,0:T(8,128)(2,1)S(1)} %copy-done, bf16[16384,1024]{1,0:T(8,128)(2,1)} %param.11), kind=kOutput, calls=%fused_computation.15 | convolution fusion | flops 4295098368 | bytes 38010880 | tf_op jit(solution)/shard_map/dot_general | solution.py:35
  68.3 0.0 copy-start.1
  68.4 0.0 copy-start.2
  68.4 0.0 copy-done.3
  68.4 0.1 dynamic_slice.15
  68.5 0.1 iota_compare_fusion
  68.6 0.0 all-to-all-done
  68.6 0.1 copy.17
  68.7 0.4 fusion.21
  69.1 5.8 %fusion.4 = (f32[16,8,16]{2,1,0:T(8,128)S(1)}, f32[16,8,16,256]{3,2,1,0:T(8,128)S(1)}) fusion(pred[16,256]{1,0:T(8,128)(4,1)S(1)} %iota_compare_fusion, bf16[128,8,256,128]{3,2,1,0:T(8,128)(2,1)} %param.13, s32[]{:T(128)S(6)} %select_n.5, bf16[16,8,16,128]{3,2,0,1:T(8,128)(2,1)S(1)} %bitcast.34), kind=kOutput, calls=%fused_computation.8 | convolution fusion | flops 135788544 | bytes 11022340 | tf_op jit(solution)/shard_map/bgrd,bgtd->bgrt/dot_general | solution.py:9
  74.8 0.0 copy-done.1
  74.8 0.0 copy-done.2
  74.9 0.9 fusion.5
  75.8 4.8 %divide_convert_fusion = bf16[16,8,16,128]{3,2,1,0:T(8,128)(2,1)S(1)} fusion(bf16[128,8,256,128]{3,2,1,0:T(8,128)(2,1)} %param.14, s32[]{:T(128)S(6)} %select_n.5, f32[16,8,16,256]{3,2,1,0:T(8,128)S(1)} %get-tuple-element.6, f32[16,8,16]{2,1,0:T(8,128)S(1)} %multiply_maximum_fusion, pred[16,256]{1,0:T(8,128)(4,1)S(1)} %iota_compare_fusion, ...), kind=kOutput, calls=%fused_computation.16 | convolution fusion | flops 137363456 | bytes 11104260 | tf_op jit(solution)/shard_map/bgrt,bgtd->bgrd/dot_general | solution.py:18
  80.7 0.2 all_to_all.29
  80.9 0.3 copy.13
  81.2 14.1 %all_to_all.35 = bf16[16,8,2048]{2,0,1:T(8,128)(2,1)S(1)} all-to-all(bf16[16,8,2048]{2,0,1:T(8,128)(2,1)S(1)} %copy.13), channel_id=1, replica_groups=mesh['replica'=2,'model'=8] {'model'}, dimensions={1} | all-to-all | bytes 1048576 | tf_op jit(solution)/shard_map/all_to_all | solution.py:45
  95.3 26.0 %fusion.30 = f32[128,16384]{1,0:T(8,128)} fusion(bf16[128,2048]{1,0:T(8,128)(2,1)S(1)} %bitcast.31, bf16[2048,16384]{1,0:T(8,128)(2,1)} %param.12), kind=kOutput, calls=%fused_computation.36 | convolution fusion | flops 8589934592 | bytes 76021760 | tf_op jit(solution)/shard_map/dot_general | solution.py:46
  121.4 0.1 all-reduce.2.cloned.1.call-update
  121.5 96.1 %all-reduce.2.cloned.1.call-done = f32[128,16384]{1,0:T(8,128)} async-done(((f32[128,16384]{1,0:T(8,128)}), f32[128,16384]{1,0:T(8,128)}) %all-reduce.2.cloned.1.call-update) | async-done | bytes 8388624 | tf_op jit(solution)/shard_map/psum | solution.py:47
  217.6 7.4 %add_convert_fusion = bf16[128,16384]{1,0:T(8,128)(2,1)} fusion(f32[128,16384]{1,0:T(8,128)} %all-reduce.2.cloned.1.call-done, bf16[128,16384]{1,0:T(8,128)(2,1)} %param.8), kind=kLoop, calls=%fused_computation | loop fusion | flops 6291456 | bytes 16777216 | tf_op jit(solution)/shard_map/convert_element_type | solution.py:48
  (6 shorter events, 0.1 us)
Async XLA Ops:
  32.7 35.8 %all-to-all-start = ((bf16[8,16,2048]{2,1,0:T(8,128)(2,1)}), bf16[8,16,2048]{2,1,0:T(8,128)(2,1)S(1)}, u32[]{:S(2)}, u32[]{:S(2)}) async-start(bf16[8,16,2048]{2,1,0:T(8,128)(2,1)} %bitcast), calls=%async_computation | async-start | bytes 1048576 | tf_op jit(solution)/shard_map/all_to_all | solution.py:33
  38.8 178.8 %all-reduce.2.cloned.1.call-start = ((), (), s32[]{:S(2)}) async-start(), calls=%async_computation.2 | async-start | bytes 16777216 | tf_op jit(solution)/shard_map/psum | solution.py:47
  38.8 16.5 %copy-start = (bf16[128,16384]{1,0:T(8,128)(2,1)S(1)}, bf16[128,16384]{1,0:T(8,128)(2,1)}, u32[]{:S(2)}) copy-start(bf16[128,16384]{1,0:T(8,128)(2,1)} %param.8) | copy-start | bytes 12582916
  55.2 13.1 %copy-start.3 = (s32[128]{0:T(128)S(1)}, s32[128]{0:T(128)}, u32[]{:S(2)}) copy-start(s32[128]{0:T(128)} %param.15) | copy-start | bytes 1540
  68.3 6.5 %copy-start.1 = (bf16[16,8,8,128]{3,2,1,0:T(8,128)(2,1)}, bf16[16,8,8,128]{3,2,1,0:T(8,128)(2,1)S(1)}, u32[]{:S(2)}) copy-start(bf16[16,8,8,128]{3,2,1,0:T(8,128)(2,1)S(1)} %copy.18) | copy-start | bytes 786436
  68.4 6.5 %copy-start.2 = (bf16[16,8,8,128]{3,2,1,0:T(8,128)(2,1)}, bf16[16,8,8,128]{3,2,1,0:T(8,128)(2,1)S(1)}, u32[]{:S(2)}) copy-start(bf16[16,8,8,128]{3,2,1,0:T(8,128)(2,1)S(1)} %copy.19) | copy-start | bytes 786436
Sparse Core Ops, SparseCore 0:
  121.6 95.9 all-reduce.1
where the time goes:
time: 232 us
  waiting for transfers between devices  96.2 us (41%)
  matrix products  92 us (40%)
  between operations  14.2 us (6%)
  blocking collectives  14.1 us (6%)
  other arithmetic  8.47 us (4%)
  starting transfers between devices  6.02 us (3%)
    psum x1, waiting for transfers between devices, local_step(): full_sum = lax.psum(part_sum, 'model')  96.1 us
    dot_general x1, matrix products, local_step(): part_sum = jnp.dot(out_heads, w_out, preferred_element_type=jnp.float32)  26 us
    dot_general x1, matrix products, local_step(): jnp.dot(x, w_query, preferred_element_type=jnp.float32).astype(jnp.bfloat16)  25.6 us
    dot_general x1, matrix products, local_step(): jnp.dot(x, w_key, preferred_element_type=jnp.float32).astype(jnp.bfloat16)  16.4 us
    all_to_all x1, blocking collectives, local_step(): lax.all_to_all(out_rows.reshape(local_rows, -1), 'model', 1, 0, tiled=True)  14.1 us
    dot_general x1, matrix products, local_step(): jnp.dot(x, w_value, preferred_element_type=jnp.float32).astype(jnp.bfloat16)  13 us
    convert_element_type x1, other arithmetic, local_step(): y = (x.astype(jnp.float32) + full_sum).astype(jnp.bfloat16)  7.41 us
    all_to_all x1, starting transfers between devices, local_step(): q_rows = lax.all_to_all(q_local, 'model', 0, 1, tiled=True)  6.01 us
  transfers between devices with their start and end apart: 2, of which 1 were waited for; matrix products, arithmetic and copies ran while one was open for 13% of the time, Pallas kernels for 0%

commit v1 on v0

v1 whole, which is shorter than its diff:
```python
import functools

import jax
import jax.numpy as jnp
from jax import lax
from jax.experimental import pallas as pl
from jax.experimental.pallas import tpu as pltpu
from jax.sharding import PartitionSpec as P

MESH = pl.DeviceIdType.MESH
CORES = 2
ROUNDS = 8
OFFSETS = (2, 1, 3, 0)
BF16 = jnp.bfloat16
F32 = jnp.float32


def attend(queries, k_rows, v_rows, k_one, v_one, seq_lens):
    inv_sqrt = queries.shape[-1] ** -0.5
    scores = jnp.einsum("brd,btd->brt", queries, k_rows, preferred_element_type=F32) * inv_sqrt
    score_new = jnp.einsum("brd,bd->br", queries, k_one, preferred_element_type=F32) * inv_sqrt
    positions = jnp.arange(k_rows.shape[1])
    in_range = positions[None, None, :] < seq_lens[:, None, None]
    scores = jnp.where(in_range, scores, -jnp.inf)
    row_max = jnp.maximum(jnp.max(scores, axis=-1), score_new)
    weights = jnp.exp(scores - row_max[..., None])
    weight_new = jnp.exp(score_new - row_max)
    norm_sum = jnp.sum(weights, axis=-1) + weight_new
    out_sum = jnp.einsum("brt,btd->brd", weights.astype(BF16), v_rows, preferred_element_type=F32)
    out_sum = out_sum + weight_new.astype(BF16).astype(F32)[..., None] * v_one.astype(F32)[:, None, :]
    return (out_sum / norm_sum[..., None]).astype(BF16)


def out_kernel(size, o_ref, kv_ref, x_ref, w_ref, y_ref, kvs_ref,
               wbuf, xbuf, part, pair, hop, near,
               w_sem, x_sem, kv_sem, pair_send, pair_recv, hop_send, hop_recv, near_send, near_recv,
               ag_send, ag_recv, fwd_send, fwd_recv):
    me = lax.axis_index("model")
    core = lax.rem(me, CORES)
    chip = me // CORES
    chips = size // CORES
    plus = lax.rem(me + CORES, size)
    minus = lax.rem(me + size - CORES, size)
    mate = me + 1 - 2 * core
    plus2 = lax.rem(me + 2 * CORES, size)
    rows, depth = o_ref.shape
    half = rows // 2
    n, nk = part.shape[-1], kv_ref.shape[1]
    width = n * size
    top, bottom = pl.ds(0, half), pl.ds(half, half)
    kv_round = ROUNDS

    def slab(r, j):
        dest = lax.rem(chip + OFFSETS[j], chips)
        cols = pl.ds(pl.multiple_of(r * width + dest * (CORES * n), CORES * n), CORES * n)
        return pltpu.make_async_copy(w_ref.at[:, cols], wbuf.at[j], w_sem.at[j])

    def own_x(r):
        cols = pl.ds(pl.multiple_of(r * width + me * n, n), n)
        return pltpu.make_async_copy(x_ref.at[:, cols], xbuf.at[r], x_sem.at[r])

    def remote(src, dst, send, recv, to):
        return pltpu.make_async_remote_copy(
            src_ref=src, dst_ref=dst, send_sem=send, recv_sem=recv,
            device_id={"model": to}, device_id_type=MESH)

    def pair_copy(r, j):
        return remote(part.at[r, j, 1 - core], pair.at[r, j], pair_send.at[r, j], pair_recv.at[r, j], mate)

    def hop_copy(r, way):
        to, lines = ((plus, top), (minus, bottom))[way]
        return remote(part.at[r, 0, core, lines], hop.at[r, way], hop_send.at[r, way], hop_recv.at[r, way], to)

    def near_copy(r, way, late):
        to = (plus, minus)[way]
        lines = top if (way == 0) == late else bottom
        k = 2 * way + int(late)
        return remote(part.at[r, 1 + way, core, lines], near.at[r, way, lines],
                      near_send.at[r, k], near_recv.at[r, k], to)

    def block(r, owner, lines):
        if r is None:
            return kvs_ref.at[lines, pl.ds(pl.multiple_of(owner * nk, nk), nk)]
        return y_ref.at[lines, pl.ds(pl.multiple_of(r * width + owner * n, n), n)]

    everything = pl.ds(0, rows)

    def gather_copy(r, k):
        i = kv_round if r is None else r
        ref = block(r, me, everything)
        return remote(ref, ref, ag_send.at[i, k], ag_recv.at[i, k], (mate, plus, minus)[k])

    def relay_copy(r, way):
        i = kv_round if r is None else r
        ref = block(r, (minus, plus)[way], (top, bottom)[way])
        return remote(ref, ref, ag_send.at[i, 3 + way], ag_recv.at[i, 3 + way], (plus, minus)[way])

    def relayed_recv(r, way):
        i = kv_round if r is None else r
        ref = block(r, plus2, (top, bottom)[way])
        return remote(ref, ref, ag_send.at[i, 3 + way], ag_recv.at[i, 3 + way], (plus, minus)[way])

    def received(r, k):
        i = kv_round if r is None else r
        ref = block(r, (mate, minus, plus)[k], everything)
        return remote(ref, ref, ag_send.at[i, k], ag_recv.at[i, k], (mate, plus, minus)[k])

    def fwd_copy(r, k):
        i = kv_round if r is None else r
        owner, lines = ((minus, everything), (plus, everything), (plus2, top), (plus2, bottom))[k]
        ref = block(r, owner, lines)
        return remote(ref, ref, fwd_send.at[i, k], fwd_recv.at[i, k], mate)

    def fwd_recv_copy(r, k):
        i = kv_round if r is None else r
        flip = 1 - 2 * core
        owner, lines = ((minus, everything), (plus, everything), (plus2, top), (plus2, bottom))[k]
        ref = block(r, owner + flip, lines)
        return remote(ref, ref, fwd_send.at[i, k], fwd_recv.at[i, k], mate)

    for j in range(4):
        slab(0, j).start()
    own_kv = pltpu.make_async_copy(kv_ref, kvs_ref.at[:, pl.ds(pl.multiple_of(me * nk, nk), nk)], kv_sem)
    own_kv.start()

    barrier = pltpu.get_barrier_semaphore()
    for to in (mate, plus, minus):
        pl.semaphore_signal(barrier, inc=1, device_id={"model": to}, device_id_type=MESH)

    @pl.loop(0, ROUNDS)
    def _(r):
        own_x(r).start()

    own_kv.wait()
    pl.semaphore_wait(barrier, 3)
    for k in range(3):
        gather_copy(None, k).start()

    def pair_sum(r, j):
        pair_copy(r, j).wait_recv()
        part[r, j, core] = part[r, j, core] + pair[r, j]
        if j == 0:
            for way in range(2):
                hop_copy(r, way).start()
        elif j < 3:
            near_copy(r, j - 1, False).start()

    def add_hops(r):
        for way in range(2):
            hop_copy(r, way).wait_recv()
            lines = (top, bottom)[way]
            part[r, 1 + way, core, lines] = part[r, 1 + way, core, lines] + hop[r, way]
            near_copy(r, way, True).start()

    def relay(r):
        for way in range(2):
            received(r, 1 + way).wait_recv()
            relay_copy(r, way).start()
            fwd_copy(r, way).start()

    def pass_far(r):
        for way in range(2):
            relayed_recv(r, way).wait_recv()
            fwd_copy(r, 2 + way).start()

    @pl.loop(0, ROUNDS)
    def _(r):
        for j in range(4):
            slab(r, j).wait()
            product = jnp.dot(o_ref[...], wbuf[j], preferred_element_type=F32)
            for q in range(CORES):
                part[r, j, q] = product[:, q * n:(q + 1) * n]
            pair_copy(r, j).start()

            @pl.when(r < ROUNDS - 1)
            def _():
                slab(r + 1, j).start()

            if j >= 2:
                pair_sum(r, j - 2)
            else:
                @pl.when(r >= 1)
                def _():
                    pair_sum(r - 1, j + 2)

        @pl.when(r == 0)
        def _():
            relay(None)

        @pl.when(r == 2)
        def _():
            pass_far(None)

        @pl.when(r >= 2)
        def _():
            add_hops(r - 2)

    for j in (2, 3):
        pair_sum(ROUNDS - 1, j)
    for r in (ROUNDS - 2, ROUNDS - 1):
        add_hops(r)

    def finish(r):
        for way in range(2):
            for late in (False, True):
                near_copy(r, way, late).wait_recv()
        own_x(r).wait()
        total = part[r, 3, core] + (near[r, 0] + near[r, 1])
        total = xbuf[r].astype(F32) + total
        y_ref[:, pl.ds(pl.multiple_of(r * width + me * n, n), n)] = total.astype(BF16)
        for k in range(3):
            gather_copy(r, k).start()

    @pl.loop(0, ROUNDS + 4)
    def _(i):
        @pl.when(i < ROUNDS)
        def _():
            finish(i)

        @pl.when((i >= 2) & (i < ROUNDS + 2))
        def _():
            relay(i - 2)

        @pl.when(i >= 4)
        def _():
            pass_far(i - 4)

    def drain(r):
        received(r, 0).wait_recv()
        for k in range(4):
            fwd_recv_copy(r, k).wait_recv()
        for k in range(3):
            gather_copy(r, k).wait_send()
        for way in range(2):
            relay_copy(r, way).wait_send()
        for k in range(4):
            fwd_copy(r, k).wait_send()

    @pl.loop(0, ROUNDS)
    def _(r):
        for j in range(4):
            pair_copy(r, j).wait_send()
        for way in range(2):
            hop_copy(r, way).wait_send()
            for late in (False, True):
                near_copy(r, way, late).wait_send()
        drain(r)

    drain(None)


def out_product(size, o, kv, x, w_out):
    rows, depth = o.shape
    model = w_out.shape[1]
    n = model // (ROUNDS * size)
    sem = pltpu.SemaphoreType.DMA
    return pl.pallas_call(
        functools.partial(out_kernel, size),
        out_shape=(pltpu.VMEM((rows, model), BF16), pltpu.VMEM((rows, size * kv.shape[1]), BF16)),
        in_specs=[
            pl.BlockSpec(memory_space=pltpu.VMEM),
            pl.BlockSpec(memory_space=pl.ANY),
            pl.BlockSpec(memory_space=pl.ANY),
            pl.BlockSpec(memory_space=pl.ANY),
        ],
        out_specs=(pl.BlockSpec(memory_space=pltpu.VMEM), pl.BlockSpec(memory_space=pltpu.VMEM)),
        scratch_shapes=[
            pltpu.VMEM((4, depth, CORES * n), BF16),
            pltpu.VMEM((ROUNDS, rows, n), BF16),
            pltpu.VMEM((ROUNDS, 4, CORES, rows, n), F32),
            pltpu.VMEM((ROUNDS, 4, rows, n), F32),
            pltpu.VMEM((ROUNDS, 2, rows // 2, n), F32),
            pltpu.VMEM((ROUNDS, 2, rows, n), F32),
            sem((4,)), sem((ROUNDS,)), sem,
            sem((ROUNDS, 4)), sem((ROUNDS, 4)),
            sem((ROUNDS, 2)), sem((ROUNDS, 2)),
            sem((ROUNDS, 4)), sem((ROUNDS, 4)),
            sem((ROUNDS + 1, 5)), sem((ROUNDS + 1, 5)),
            sem((ROUNDS + 1, 4)), sem((ROUNDS + 1, 4)),
        ],
        compiler_params=pltpu.CompilerParams(
            collective_id=0, has_side_effects=True, vmem_limit_bytes=48 * 1024 * 1024),
        cost_estimate=pl.CostEstimate(
            flops=2 * rows * depth * model, bytes_accessed=depth * model * 2, transcendentals=0),
        name="out_reduce",
    )(o, kv, x, w_out)


def solution(mesh):
    size = mesh.shape["model"]

    def local_step(x, w_query, w_key, w_value, w_out, k_cache, v_cache, lengths):
        rows = x.shape[0]
        head_dim = k_cache.shape[3]
        kv_heads = k_cache.shape[1]
        me = lax.axis_index("model")
        q = jnp.dot(x, w_query, preferred_element_type=F32).astype(BF16)
        wk = lax.dynamic_slice_in_dim(w_key, me * head_dim, head_dim, axis=1)
        wv = lax.dynamic_slice_in_dim(w_value, me * head_dim, head_dim, axis=1)
        k_one = jnp.dot(x, wk, preferred_element_type=F32).astype(BF16)
        v_one = jnp.dot(x, wv, preferred_element_type=F32).astype(BF16)
        out = attend(
            q.reshape(rows, -1, head_dim),
            lax.dynamic_index_in_dim(k_cache, me, axis=1, keepdims=False),
            lax.dynamic_index_in_dim(v_cache, me, axis=1, keepdims=False),
            k_one, v_one, lengths)
        kv = jnp.concatenate([k_one, v_one], axis=1)
        y, kvs = out_product(size, out.reshape(rows, -1), kv, x, w_out)
        kvs = kvs.reshape(rows, kv_heads, 2, head_dim)
        return y, kvs[:, :, 0], kvs[:, :, 1]

    rows_spec = P("replica")
    return jax.shard_map(
        local_step,
        mesh=mesh,
        in_specs=(P("replica", None), P(None, "model"), P(), P(), P("model", None), rows_spec, rows_spec, rows_spec),
        out_specs=(rows_spec, rows_spec, rows_spec),
        check_vma=False,
    )
```

time: 232 us -> 116 us (0.50)
  waiting for transfers between devices: 96.2 us -> 0 us
  Pallas kernels: 0 us -> 65 us
  matrix products: 92 us -> 44.4 us
  blocking collectives: 14.1 us -> 0 us
  between operations: 14.2 us -> 0.74 us
  other arithmetic: 8.47 us -> 1.9 us
  starting transfers between devices: 6.02 us -> 0 us
  local copies, waits for them, and re-layouts: 0.83 us -> 4.23 us
    psum x1 -> x0, waiting for transfers between devices: 96.1 us -> none  [local_step(): full_sum = lax.psum(part_sum, 'model')]
    pallas_call x0 -> x1, Pallas kernels: none -> 65 us  [out_product(): pl.pallas_call(functools.partial(out_kernel, size), out_shape=(pltpu.VMEM...]
    dot_general x7 -> x6, matrix products: 92 us -> 44.4 us  [the longest x1 25 us: local_step(): q = jnp.dot(x, w_query, preferred_element_type=F32).astype(BF16)]
    all_to_all x1 -> x0, blocking collectives: 14.1 us -> none  [local_step(): lax.all_to_all(out_rows.reshape(local_rows, -1), 'model', 1, 0, tiled=True)]
    convert_element_type x3 -> x1, other arithmetic: 7.44 us -> 0.02 us  [attend(): weight_new.astype(BF16).astype(F32)[..., None]]
    all_to_all x1 -> x0, starting transfers between devices: 6.01 us -> none  [local_step(): q_rows = lax.all_to_all(q_local, 'model', 0, 1, tiled=True)]
  transfers between devices with their start and end apart: 2 -> 0, of which waited for: 1 -> 0; matrix products, arithmetic and copies ran while one was open for 13% -> 0% of each run, Pallas kernels for 0% -> 0%
where the time goes in v1:
time: 116 us
  Pallas kernels  65 us (56%)
  matrix products  44.4 us (38%)
  local copies, waits for them, and re-layouts  4.23 us (4%)
  other arithmetic  1.9 us (2%)
    pallas_call x1, Pallas kernels, out_product(): pl.pallas_call(functools.partial(out_kernel, size), out_shape=(pltpu.VMEM...  65 us
    dot_general x1, matrix products, local_step(): q = jnp.dot(x, w_query, preferred_element_type=F32).astype(BF16)  25 us
    dot_general x1, matrix products, attend(): jnp.einsum('brd,btd->brt', queries, k_rows, preferred_element_type=F32)  5.77 us
    dot_general x1, matrix products, attend(): jnp.einsum('brt,btd->brd', weights.astype(BF16), v_rows, preferred_elemen...  4.9 us
    dot_general x1, matrix products, local_step(): k_one = jnp.dot(x, wk, preferred_element_type=F32).astype(BF16)  4.85 us
    dot_general x1, matrix products, local_step(): v_one = jnp.dot(x, wv, preferred_element_type=F32).astype(BF16)  3.54 us

profile of v1, /device:TPU:113, one launch (start us, length us, event | category | flops | bytes accessed | tf_op | source)
XLA Modules:
  0.0 116.3 jit_solution(12720066037546134405)
XLA Ops:
  0.6 0.7 iota_compare_fusion
  1.4 0.0 copy-start
  1.4 4.9 %fusion.17 = bf16[128,128]{0,1:T(8,128)(2,1)S(1)} fusion(bf16[128,16384]{1,0:T(8,128)(2,1)} %x_ref.1, bf16[16384,1024]{1,0:T(8,128)(2,1)} %param.10, s32[]{:T(128)S(6)} %select_n.15), kind=kOutput, calls=%fused_computation.18 | convolution fusion | flops 536887296 | bytes 8421380 | tf_op jit(solution)/shard_map/dot_general | solution.py:300
  6.2 0.0 copy-done
  6.3 3.5 %fusion.45 = (f32[128,128]{1,0:T(8,128)S(1)}, bf16[128,128]{1,0:T(8,128)(2,1)S(1)}) fusion(bf16[128,16384]{1,0:T(8,128)(2,1)S(1)} %copy-done, bf16[16384,1024]{1,0:T(8,128)(2,1)} %param.11, s32[]{:T(128)S(6)} %select_n.15), kind=kOutput, calls=%fused_computation.44 | convolution fusion | flops 536903680 | bytes 8486916 | tf_op jit(solution)/shard_map/dot_general | solution.py:301
  9.8 25.0 %fusion.16 = bf16[16,8,16,128]{3,1,2,0:T(8,128)(2,1)S(1)} fusion(bf16[128,16384]{1,0:T(8,128)(2,1)} %x_ref.1, bf16[16384,2048]{1,0:T(8,128)(2,1)} %param.9), kind=kOutput, calls=%fused_computation.17 | convolution fusion | flops 8590196736 | bytes 71827456 | tf_op jit(solution)/shard_map/dot_general | solution.py:297
  34.8 0.1 copy.21
  34.9 0.4 fusion.35
  35.3 5.8 %fusion.10 = (f32[128,16]{1,0:T(8,128)S(1)}, f32[128,16,256]{2,1,0:T(8,128)S(1)}) fusion(pred[128,256]{1,0:T(8,128)(4,1)S(1)} %iota_compare_fusion, bf16[128,16,128]{2,1,0:T(8,128)(2,1)S(1)} %bitcast.38, bf16[128,8,256,128]{3,2,1,0:T(8,128)(2,1)} %param.13, s32[]{:T(128)S(6)} %select_n.13), kind=kOutput, calls=%fused_computation.13 | convolution fusion | flops 135788544 | bytes 11051012 | tf_op jit(solution)/shard_map/brd,btd->brt/dot_general | solution.py:20
  41.1 1.1 fusion.11
  42.2 4.9 %divide_convert_fusion = bf16[128,16,128]{2,1,0:T(8,128)(2,1)S(1)} fusion(bf16[128,8,256,128]{3,2,1,0:T(8,128)(2,1)} %param.14, s32[]{:T(128)S(6)} %select_n.13, f32[128,16,256]{2,1,0:T(8,128)S(1)} %get-tuple-element.12, f32[128,16]{1,0:T(8,128)S(1)} %multiply_maximum_fusion, pred[128,256]{1,0:T(8,128)(4,1)S(1)} %iota_compare_fusion, ...), kind=kOutput, calls=%fused_computation.21 | convolution fusion | flops 137363456 | bytes 11132932 | tf_op jit(solution)/shard_map/brt,btd->brd/dot_general | solution.py:29
  47.1 0.1 copy.28
  47.3 65.0 %out_reduce.1 = (bf16[128,16384]{1,0:T(8,128)(2,1)S(1)}, bf16[128,2048]{1,0:T(8,128)(2,1)S(1)}) custom-call(bf16[128,2048]{1,0:T(8,128)(2,1)S(1)} %bitcast.36, bf16[128,256]{1,0:T(8,128)(2,1)S(1)} %pad_maximum_fusion.kv_ref, bf16[128,16384]{1,0:T(8,128)(2,1)} %x_ref.1, bf16[2048,16384]{1,0:T(8,128)(2,1)} %w_ref.1), custom_call_target="tpu_custom_call" | custom-call | flops 8589934592 | bytes 67108864 | tf_op jit(solution)/shard_map/out_reduce/pallas_call | solution.py:257
  112.3 2.0 %copy.30 = bf16[128,16384]{1,0:T(8,128)(2,1)} copy(bf16[128,16384]{1,0:T(8,128)(2,1)S(1)} %get-tuple-element.17) | data formatting | bytes 8388608
  114.3 0.4 reshape.42
  114.7 0.7 fusion.44
  115.4 0.9 copy_bitcast_fusion.1
  (3 shorter events, 0.1 us)
Async XLA Ops:
  1.4 4.9 %copy-start = (bf16[128,16384]{1,0:T(8,128)(2,1)S(1)}, bf16[128,16384]{1,0:T(8,128)(2,1)}, u32[]{:S(2)}) copy-start(bf16[128,16384]{1,0:T(8,128)(2,1)} %x_ref.1) | copy-start | bytes 12582916

commit v2 on v1

--- a/solution.py
+++ b/solution.py
@@ -10,25 +10,193 @@
 MESH = pl.DeviceIdType.MESH
 CORES = 2
 ROUNDS = 8
+DEPTH = 512
+SHORT = 32
+LONG_STEP = 4
 OFFSETS = (2, 1, 3, 0)
 BF16 = jnp.bfloat16
 F32 = jnp.float32
 
 
-def attend(queries, k_rows, v_rows, k_one, v_one, seq_lens):
-    inv_sqrt = queries.shape[-1] ** -0.5
-    scores = jnp.einsum("brd,btd->brt", queries, k_rows, preferred_element_type=F32) * inv_sqrt
-    score_new = jnp.einsum("brd,bd->br", queries, k_one, preferred_element_type=F32) * inv_sqrt
-    positions = jnp.arange(k_rows.shape[1])
-    in_range = positions[None, None, :] < seq_lens[:, None, None]
-    scores = jnp.where(in_range, scores, -jnp.inf)
-    row_max = jnp.maximum(jnp.max(scores, axis=-1), score_new)
-    weights = jnp.exp(scores - row_max[..., None])
-    weight_new = jnp.exp(score_new - row_max)
-    norm_sum = jnp.sum(weights, axis=-1) + weight_new
-    out_sum = jnp.einsum("brt,btd->brd", weights.astype(BF16), v_rows, preferred_element_type=F32)
-    out_sum = out_sum + weight_new.astype(BF16).astype(F32)[..., None] * v_one.astype(F32)[:, None, :]
-    return (out_sum / norm_sum[..., None]).astype(BF16)
+def front_kernel(x_ref, wq_ref, wk_ref, wv_ref, kc_ref, vc_ref, len_ref, o_ref, kv_ref,
+                 xbuf, wbuf, acc, qbuf, obuf, kshort, vshort, klong, vlong, lens, order,
+                 x_sem, w_sem, short_sem, long_sem, len_sem):
+    me = lax.axis_index("model")
+    steps, rows, depth = xbuf.shape
+    slots = wbuf.shape[0]
+    heads, dim = qbuf.shape[1:]
+    width = heads * dim
+    context = klong.shape[1]
+    unit = context // SHORT
+    per_step = rows // steps
+    head_cols = pl.ds(pl.multiple_of(me * dim, dim), dim)
+
+    def x_copy(s):
+        cols = pl.ds(pl.multiple_of(s * depth, depth), depth)
+        return pltpu.make_async_copy(x_ref.at[:, cols], xbuf.at[s], x_sem.at[s])
+
+    def w_copies(s, slot):
+        lines = pl.ds(pl.multiple_of(s * depth, depth), depth)
+        return (
+            pltpu.make_async_copy(wq_ref.at[lines], wbuf.at[slot, :, pl.ds(0, width)], w_sem.at[slot, 0]),
+            pltpu.make_async_copy(wk_ref.at[lines, head_cols], wbuf.at[slot, :, pl.ds(width, dim)], w_sem.at[slot, 1]),
+            pltpu.make_async_copy(wv_ref.at[lines, head_cols], wbuf.at[slot, :, pl.ds(width + dim, dim)], w_sem.at[slot, 2]),
+        )
+
+    def short_copies():
+        lines = pl.ds(0, SHORT)
+        return (pltpu.make_async_copy(kc_ref.at[:, me, lines], kshort, short_sem.at[0]),
+                pltpu.make_async_copy(vc_ref.at[:, me, lines], vshort, short_sem.at[1]))
+
+    def long_copies(b, slot):
+        return (pltpu.make_async_copy(kc_ref.at[b, me], klong.at[slot], long_sem.at[0]),
+                pltpu.make_async_copy(vc_ref.at[b, me], vlong.at[slot], long_sem.at[1]))
+
+    len_copy = pltpu.make_async_copy(len_ref, lens, len_sem)
+    for s in range(slots):
+        x_copy(s).start()
+        for copy in w_copies(s, s):
+            copy.start()
+        if s == 0:
+            len_copy.start()
+
+    @pl.loop(slots, steps)
+    def _(s):
+        x_copy(s).start()
+
+    acc[...] = jnp.zeros_like(acc)
+    len_copy.wait()
+
+    def stream(s, count):
+        slot = lax.rem(s, slots)
+        x_copy(s).wait()
+        for copy in w_copies(s, slot):
+            copy.wait()
+        acc[...] += jnp.dot(xbuf[s], wbuf[slot], preferred_element_type=F32)
+
+        @pl.when(s + slots < steps)
+        def _():
+            for copy in w_copies(s + slots, slot):
+                copy.start()
+
+        @pl.when(s == steps // 4)
+        def _():
+            for copy in short_copies():
+                copy.start()
+
+        for i in range(per_step):
+            b = s * per_step + i
+            is_long = lens[b] > SHORT
+
+            @pl.when(is_long)
+            def _():
+                order[count] = b
+                for copy in long_copies(b, count):
+                    copy.start()
+
+            count = count + is_long.astype(jnp.int32)
+        return count
+
+    count = lax.fori_loop(0, steps, stream, jnp.int32(0))
+
+    for h in range(heads):
+        qbuf[:, h, :] = acc[:, h * dim:(h + 1) * dim].astype(BF16).astype(F32)
+    kv_ref[...] = acc[:, width:].astype(BF16)
+    for copy in short_copies():
+        copy.wait()
+
+    inv_sqrt = dim ** -0.5
+    contract_last = (((1,), (1,)), ((), ()))
+
+    def attend(q, keys, values, valid, valid_new):
+        scores = lax.dot_general(q, keys, contract_last, preferred_element_type=F32) * inv_sqrt
+        score_new = lax.dot_general(q, kv_ref[:, :dim], contract_last, preferred_element_type=F32) * inv_sqrt
+        scores = jnp.where(valid, scores, -jnp.inf)
+        score_new = jnp.where(valid_new, score_new, -jnp.inf)
+        row_max = jnp.maximum(jnp.max(scores, axis=-1, keepdims=True), jnp.max(score_new, axis=-1, keepdims=True))
+        weights = jnp.exp(scores - row_max)
+        weight_new = jnp.exp(score_new - row_max)
+        norm = jnp.sum(weights, axis=-1, keepdims=True) + jnp.sum(weight_new, axis=-1, keepdims=True)
+        total = jnp.dot(weights.astype(BF16), values, preferred_element_type=F32)
+        total = total + jnp.dot(weight_new.astype(BF16), kv_ref[:, dim:], preferred_element_type=F32)
+        return total / norm
+
+    def iota(shape, axis):
+        return lax.broadcasted_iota(jnp.int32, shape, axis)
+
+    short_rows = unit * heads
+    row_seq = iota((short_rows, 1), 0) // heads
+    col = iota((short_rows, context), 1)
+    place = jnp.where(col // SHORT == row_seq, col % SHORT, context)
+    new_seq = iota((short_rows, rows), 1) - row_seq
+    line = iota((1, context), 1)
+
+    @pl.loop(0, rows // unit // 2)
+    def _(pair):
+        for i in range(2):
+            first = (pair * 2 + i) * unit
+            bound = jnp.zeros((1, context), jnp.int32)
+            for j in range(unit):
+                bound = jnp.where(line // SHORT == j, lens[first + j], bound)
+            seqs = pl.ds(pl.multiple_of(first, unit), unit)
+            out = attend(
+                qbuf[seqs].reshape(short_rows, dim).astype(BF16),
+                kshort[seqs].reshape(context, dim), vshort[seqs].reshape(context, dim),
+                place < bound, new_seq == first)
+            obuf[seqs] = out.reshape(unit, heads, dim)
+
+    @pl.loop(0, count)
+    def _(i):
+        for copy in long_copies(0, 0):
+            copy.wait()
+
+    long_col = iota((heads, context), 1)
+    long_seq = iota((heads, rows), 1)
+
+    @pl.loop(0, (count + LONG_STEP - 1) // LONG_STEP)
+    def _(i):
+        for j in range(LONG_STEP):
+            slot = jnp.minimum(i * LONG_STEP + j, count - 1)
+            b = order[slot]
+            obuf[b] = attend(
+                qbuf[b].astype(BF16), klong[slot], vlong[slot], long_col < lens[b], long_seq == b)
+
+    for h in range(heads):
+        o_ref[:, h * dim:(h + 1) * dim] = obuf[:, h, :].astype(BF16)
+
+
+def front(x, w_query, w_key, w_value, k_cache, v_cache, lengths):
+    rows, model = x.shape
+    width = w_query.shape[1]
+    context, dim = k_cache.shape[2:]
+    heads = width // dim
+    steps = model // DEPTH
+    sem = pltpu.SemaphoreType.DMA
+    total = width + 2 * dim
+    return pl.pallas_call(
+        front_kernel,
+        out_shape=(pltpu.VMEM((rows, width), BF16), pltpu.VMEM((rows, 2 * dim), BF16)),
+        in_specs=[pl.BlockSpec(memory_space=pl.ANY)] * 7,
+        out_specs=(pl.BlockSpec(memory_space=pltpu.VMEM), pl.BlockSpec(memory_space=pltpu.VMEM)),
+        scratch_shapes=[
+            pltpu.VMEM((steps, rows, DEPTH), BF16),
+            pltpu.VMEM((4, DEPTH, total), BF16),
+            pltpu.VMEM((rows, total), F32),
+            pltpu.VMEM((rows, heads, dim), F32),
+            pltpu.VMEM((rows, heads, dim), F32),
+            pltpu.VMEM((rows, SHORT, dim), BF16),
+            pltpu.VMEM((rows, SHORT, dim), BF16),
+            pltpu.VMEM((rows, context, dim), BF16),
+            pltpu.VMEM((rows, context, dim), BF16),
+            pltpu.SMEM((rows,), jnp.int32),
+            pltpu.SMEM((rows,), jnp.int32),
+            sem((steps,)), sem((4, 3)), sem((2,)), sem((2,)), sem,
+        ],
+        compiler_params=pltpu.CompilerParams(vmem_limit_bytes=52 * 1024 * 1024),
+        cost_estimate=pl.CostEstimate(
+            flops=2 * rows * model * total, bytes_accessed=model * total * 2, transcendentals=0),
+        name="front",
+    )(x, w_query, w_key, w_value, k_cache, v_cache, lengths)
 
 
 def out_kernel(size, o_ref, kv_ref, x_ref, w_ref, y_ref, kvs_ref,
@@ -293,19 +461,8 @@
         rows = x.shape[0]
         head_dim = k_cache.shape[3]
         kv_heads = k_cache.shape[1]
-        me = lax.axis_index("model")
-        q = jnp.dot(x, w_query, preferred_element_type=F32).astype(BF16)
-        wk = lax.dynamic_slice_in_dim(w_key, me * head_dim, head_dim, axis=1)
-        wv = lax.dynamic_slice_in_dim(w_value, me * head_dim, head_dim, axis=1)
-        k_one = jnp.dot(x, wk, preferred_element_type=F32).astype(BF16)
-        v_one = jnp.dot(x, wv, preferred_element_type=F32).astype(BF16)
-        out = attend(
-            q.reshape(rows, -1, head_dim),
-            lax.dynamic_index_in_dim(k_cache, me, axis=1, keepdims=False),
-            lax.dynamic_index_in_dim(v_cache, me, axis=1, keepdims=False),
-            k_one, v_one, lengths)
-        kv = jnp.concatenate([k_one, v_one], axis=1)
-        y, kvs = out_product(size, out.reshape(rows, -1), kv, x, w_out)
+        out, kv = front(x, w_query, w_key, w_value, k_cache, v_cache, lengths)
+        y, kvs = out_product(size, out, kv, x, w_out)
         kvs = kvs.reshape(rows, kv_heads, 2, head_dim)
         return y, kvs[:, :, 0], kvs[:, :, 1]
 

time: 116 us -> 107 us (0.922)
  matrix products: 44.4 us -> 0 us
  Pallas kernels: 65 us -> 101 us
  other arithmetic: 1.9 us -> 0 us
    dot_general x6 -> x0, matrix products: 44.4 us -> none  [the longest x1 25 us: local_step(): q = jnp.dot(x, w_query, preferred_element_type=F32).astype(BF16)]
    pallas_call x0 -> x1, Pallas kernels: none -> 36.3 us  [front(): pl.pallas_call(front_kernel, out_shape=(pltpu.VMEM((rows, width), BF16),...]
    unnamed x5 -> x3, local copies, waits for them, and re-layouts: 2.27 us -> 2.66 us
where the time goes in v2:
time: 107 us
  Pallas kernels  101 us (94%)
  local copies, waits for them, and re-layouts  4.62 us (4%)
    pallas_call x1, Pallas kernels, out_product(): pl.pallas_call(functools.partial(out_kernel, size), out_shape=(pltpu.VMEM...  65 us
    pallas_call x1, Pallas kernels, front(): pl.pallas_call(front_kernel, out_shape=(pltpu.VMEM((rows, width), BF16),...  36.3 us
    unnamed x3, local copies, waits for them, and re-layouts  2.66 us

profile of v2, /device:TPU:113, one launch (start us, length us, event | category | flops | bytes accessed | tf_op | source)
XLA Modules:
  0.0 106.6 jit_solution(15623710080363691213)
XLA Ops:
  0.6 0.0 copy-start
  0.6 0.6 copy-done
  1.3 36.3 %front.1 = (bf16[128,2048]{1,0:T(8,128)(2,1)S(1)}, bf16[128,256]{1,0:T(8,128)(2,1)S(1)}) custom-call(bf16[128,16384]{1,0:T(8,128)(2,1)} %x_ref.3, bf16[16384,2048]{1,0:T(8,128)(2,1)} %wq_ref.1, bf16[16384,1024]{1,0:T(8,128)(2,1)} %wk_ref.1, bf16[16384,1024]{1,0:T(8,128)(2,1)} %wv_ref.1, bf16[128,8,256,128]{3,2,1,0:T(8,128)(2,1)} %kc_ref.1, ...), custom_call_target="tpu_custom_call" | custom-call | flops 9663676416 | bytes 75497472 | tf_op jit(solution)/shard_map/front/pallas_call | solution.py:176
  37.6 65.0 %out_reduce.1 = (bf16[128,16384]{1,0:T(8,128)(2,1)S(1)}, bf16[128,2048]{1,0:T(8,128)(2,1)S(1)}) custom-call(bf16[128,2048]{1,0:T(8,128)(2,1)S(1)} %get-tuple-element.7.o_ref, bf16[128,256]{1,0:T(8,128)(2,1)S(1)} %get-tuple-element.8.kv_ref, bf16[128,16384]{1,0:T(8,128)(2,1)} %x_ref.3, bf16[2048,16384]{1,0:T(8,128)(2,1)} %w_ref.1), custom_call_target="tpu_custom_call" | custom-call | flops 8589934592 | bytes 67108864 | tf_op jit(solution)/shard_map/out_reduce/pallas_call | solution.py:425
  102.6 2.0 %copy.18 = bf16[128,16384]{1,0:T(8,128)(2,1)} copy(bf16[128,16384]{1,0:T(8,128)(2,1)S(1)} %get-tuple-element.15) | data formatting | bytes 8388608
  104.7 0.4 reshape.9
  105.0 0.7 fusion
  105.8 0.9 copy_bitcast_fusion
Async XLA Ops:
  0.6 0.7 copy-start

commit v3 on v2

--- a/solution.py
+++ b/solution.py
@@ -10,16 +10,19 @@
 MESH = pl.DeviceIdType.MESH
 CORES = 2
 ROUNDS = 8
+WRITES = 8
 DEPTH = 512
 SHORT = 32
-LONG_STEP = 4
+SHORT_STEP = 4
+PACK = 16
+LONG_STEP = 10
 OFFSETS = (2, 1, 3, 0)
 BF16 = jnp.bfloat16
 F32 = jnp.float32
 
 
 def front_kernel(x_ref, wq_ref, wk_ref, wv_ref, kc_ref, vc_ref, len_ref, o_ref, kv_ref,
-                 xbuf, wbuf, acc, qbuf, obuf, kshort, vshort, klong, vlong, lens, order,
+                 xbuf, wbuf, acc, kvf, qbuf, obuf, kshort, vshort, klong, vlong, lens, order,
                  x_sem, w_sem, short_sem, long_sem, len_sem):
     me = lax.axis_index("model")
     steps, rows, depth = xbuf.shape
@@ -86,7 +89,7 @@
 
         for i in range(per_step):
             b = s * per_step + i
-            is_long = lens[b] > SHORT
+            is_long = lens[b] > SHORT - 1
 
             @pl.when(is_long)
             def _():
@@ -99,50 +102,67 @@
 
     count = lax.fori_loop(0, steps, stream, jnp.int32(0))
 
+    kv = acc[:, width:].astype(BF16)
+    kv_ref[...] = kv
+    kvf[...] = kv.astype(F32)
     for h in range(heads):
         qbuf[:, h, :] = acc[:, h * dim:(h + 1) * dim].astype(BF16).astype(F32)
-    kv_ref[...] = acc[:, width:].astype(BF16)
+
+    inv_sqrt = dim ** -0.5
+    contract_last = (((1,), (1,)), ((), ()))
+
+    def iota(shape, axis):
+        return lax.broadcasted_iota(jnp.int32, shape, axis)
+
+    is_last = iota((PACK, dim), 0) == PACK - 1
+
+    def put_new(keys, values, slot, size, b):
+        lines = pl.ds(size - PACK, PACK)
+        row = kvf[pl.ds(b, 1), :]
+        new_key = jnp.broadcast_to(row[:, :dim], (PACK, dim)).astype(BF16)
+        new_value = jnp.broadcast_to(row[:, dim:], (PACK, dim)).astype(BF16)
+        keys[slot, lines, :] = jnp.where(is_last, new_key, keys[slot, lines, :])
+        values[slot, lines, :] = jnp.where(is_last, new_value, values[slot, lines, :])
+
+    def attend(items):
+        scores = [lax.dot_general(q, keys, contract_last, preferred_element_type=F32) for q, keys, _, _ in items]
+        weights, norms = [], []
+        for score, (_, _, _, valid) in zip(scores, items):
+            score = jnp.where(valid, score * inv_sqrt, -jnp.inf)
+            weight = jnp.exp(score - jnp.max(score, axis=-1, keepdims=True))
+            norms.append(jnp.sum(weight, axis=-1, keepdims=True))
+            weights.append(weight.astype(BF16))
+        totals = [jnp.dot(weight, item[2], preferred_element_type=F32) for weight, item in zip(weights, items)]
+        return [total / norm for total, norm in zip(totals, norms)]
+
     for copy in short_copies():
         copy.wait()
 
-    inv_sqrt = dim ** -0.5
-    contract_last = (((1,), (1,)), ((), ()))
-
-    def attend(q, keys, values, valid, valid_new):
-        scores = lax.dot_general(q, keys, contract_last, preferred_element_type=F32) * inv_sqrt
-        score_new = lax.dot_general(q, kv_ref[:, :dim], contract_last, preferred_element_type=F32) * inv_sqrt
-        scores = jnp.where(valid, scores, -jnp.inf)
-        score_new = jnp.where(valid_new, score_new, -jnp.inf)
-        row_max = jnp.maximum(jnp.max(scores, axis=-1, keepdims=True), jnp.max(score_new, axis=-1, keepdims=True))
-        weights = jnp.exp(scores - row_max)
-        weight_new = jnp.exp(score_new - row_max)
-        norm = jnp.sum(weights, axis=-1, keepdims=True) + jnp.sum(weight_new, axis=-1, keepdims=True)
-        total = jnp.dot(weights.astype(BF16), values, preferred_element_type=F32)
-        total = total + jnp.dot(weight_new.astype(BF16), kv_ref[:, dim:], preferred_element_type=F32)
-        return total / norm
-
-    def iota(shape, axis):
-        return lax.broadcasted_iota(jnp.int32, shape, axis)
+    @pl.loop(0, rows // unit)
+    def _(u):
+        for j in range(unit):
+            put_new(kshort, vshort, u * unit + j, SHORT, u * unit + j)
 
     short_rows = unit * heads
-    row_seq = iota((short_rows, 1), 0) // heads
     col = iota((short_rows, context), 1)
-    place = jnp.where(col // SHORT == row_seq, col % SHORT, context)
-    new_seq = iota((short_rows, rows), 1) - row_seq
+    own = col // SHORT == iota((short_rows, 1), 0) // heads
+    place = jnp.where(own, jnp.where(col % SHORT == SHORT - 1, -1, col % SHORT), context)
     line = iota((1, context), 1)
 
-    @pl.loop(0, rows // unit // 2)
-    def _(pair):
-        for i in range(2):
-            first = (pair * 2 + i) * unit
+    @pl.loop(0, rows // unit // SHORT_STEP)
+    def _(group):
+        items, places = [], []
+        for i in range(SHORT_STEP):
+            first = (group * SHORT_STEP + i) * unit
             bound = jnp.zeros((1, context), jnp.int32)
             for j in range(unit):
                 bound = jnp.where(line // SHORT == j, lens[first + j], bound)
             seqs = pl.ds(pl.multiple_of(first, unit), unit)
-            out = attend(
+            places.append(seqs)
+            items.append((
                 qbuf[seqs].reshape(short_rows, dim).astype(BF16),
-                kshort[seqs].reshape(context, dim), vshort[seqs].reshape(context, dim),
-                place < bound, new_seq == first)
+                kshort[seqs].reshape(context, dim), vshort[seqs].reshape(context, dim), place < bound))
+        for seqs, out in zip(places, attend(items)):
             obuf[seqs] = out.reshape(unit, heads, dim)
 
     @pl.loop(0, count)
@@ -150,16 +170,21 @@
         for copy in long_copies(0, 0):
             copy.wait()
 
+    @pl.loop(0, count)
+    def _(i):
+        put_new(klong, vlong, i, context, order[i])
+
     long_col = iota((heads, context), 1)
-    long_seq = iota((heads, rows), 1)
+    long_place = jnp.where(long_col == context - 1, -1, long_col)
 
     @pl.loop(0, (count + LONG_STEP - 1) // LONG_STEP)
     def _(i):
-        for j in range(LONG_STEP):
-            slot = jnp.minimum(i * LONG_STEP + j, count - 1)
-            b = order[slot]
-            obuf[b] = attend(
-                qbuf[b].astype(BF16), klong[slot], vlong[slot], long_col < lens[b], long_seq == b)
+        slots = [jnp.minimum(i * LONG_STEP + j, count - 1) for j in range(LONG_STEP)]
+        seqs = [order[slot] for slot in slots]
+        outs = attend([(qbuf[b].astype(BF16), klong[slot], vlong[slot], long_place < lens[b])
+                       for slot, b in zip(slots, seqs)])
+        for b, out in zip(seqs, outs):
+            obuf[b] = out
 
     for h in range(heads):
         o_ref[:, h * dim:(h + 1) * dim] = obuf[:, h, :].astype(BF16)
@@ -176,12 +201,13 @@
     return pl.pallas_call(
         front_kernel,
         out_shape=(pltpu.VMEM((rows, width), BF16), pltpu.VMEM((rows, 2 * dim), BF16)),
-        in_specs=[pl.BlockSpec(memory_space=pl.ANY)] * 7,
+        in_specs=[pl.BlockSpec(memory_space=pl.ANY)] * 6 + [pl.BlockSpec(memory_space=pltpu.HBM)],
         out_specs=(pl.BlockSpec(memory_space=pltpu.VMEM), pl.BlockSpec(memory_space=pltpu.VMEM)),
         scratch_shapes=[
             pltpu.VMEM((steps, rows, DEPTH), BF16),
             pltpu.VMEM((4, DEPTH, total), BF16),
             pltpu.VMEM((rows, total), F32),
+            pltpu.VMEM((rows, 2 * dim), F32),
             pltpu.VMEM((rows, heads, dim), F32),
             pltpu.VMEM((rows, heads, dim), F32),
             pltpu.VMEM((rows, SHORT, dim), BF16),
@@ -199,8 +225,8 @@
     )(x, w_query, w_key, w_value, k_cache, v_cache, lengths)
 
 
-def out_kernel(size, o_ref, kv_ref, x_ref, w_ref, y_ref, kvs_ref,
-               wbuf, xbuf, part, pair, hop, near,
+def out_kernel(size, o_ref, kv_ref, x_ref, w_ref, y_ref, k_ref, v_ref,
+               kvs_ref, kv_heads, wbuf, xbuf, part, pair, hop, near,
                w_sem, x_sem, kv_sem, pair_send, pair_recv, hop_send, hop_recv, near_send, near_recv,
                ag_send, ag_recv, fwd_send, fwd_recv):
     me = lax.axis_index("model")
@@ -368,6 +394,24 @@
     for r in (ROUNDS - 2, ROUNDS - 1):
         add_hops(r)
 
+    def drain(r):
+        received(r, 0).wait_recv()
+        for k in range(4):
+            fwd_recv_copy(r, k).wait_recv()
+        for k in range(3):
+            gather_copy(r, k).wait_send()
+        for way in range(2):
+            relay_copy(r, way).wait_send()
+        for k in range(4):
+            fwd_copy(r, k).wait_send()
+
+    drain(None)
+    dim = nk // 2
+    for i, ref in enumerate((k_ref, v_ref)):
+        for owner in range(size):
+            kv_heads[:, owner, :] = kvs_ref[:, owner * nk + i * dim:owner * nk + (i + 1) * dim].astype(F32)
+        ref[...] = kv_heads[...].astype(BF16)
+
     def finish(r):
         for way in range(2):
             for late in (False, True):
@@ -393,17 +437,6 @@
         def _():
             pass_far(i - 4)
 
-    def drain(r):
-        received(r, 0).wait_recv()
-        for k in range(4):
-            fwd_recv_copy(r, k).wait_recv()
-        for k in range(3):
-            gather_copy(r, k).wait_send()
-        for way in range(2):
-            relay_copy(r, way).wait_send()
-        for k in range(4):
-            fwd_copy(r, k).wait_send()
-
     @pl.loop(0, ROUNDS)
     def _(r):
         for j in range(4):
@@ -414,8 +447,6 @@
                 near_copy(r, way, late).wait_send()
         drain(r)
 
-    drain(None)
-
 
 def out_product(size, o, kv, x, w_out):
     rows, depth = o.shape
@@ -424,15 +455,17 @@
     sem = pltpu.SemaphoreType.DMA
     return pl.pallas_call(
         functools.partial(out_kernel, size),
-        out_shape=(pltpu.VMEM((rows, model), BF16), pltpu.VMEM((rows, size * kv.shape[1]), BF16)),
+        out_shape=(pltpu.VMEM((rows, model), BF16),) + (pltpu.VMEM((rows, size, kv.shape[1] // 2), BF16),) * 2,
         in_specs=[
             pl.BlockSpec(memory_space=pltpu.VMEM),
             pl.BlockSpec(memory_space=pl.ANY),
             pl.BlockSpec(memory_space=pl.ANY),
             pl.BlockSpec(memory_space=pl.ANY),
         ],
-        out_specs=(pl.BlockSpec(memory_space=pltpu.VMEM), pl.BlockSpec(memory_space=pltpu.VMEM)),
+        out_specs=(pl.BlockSpec(memory_space=pltpu.VMEM),) * 3,
         scratch_shapes=[
+            pltpu.VMEM((rows, size * kv.shape[1]), BF16),
+            pltpu.VMEM((rows, size, kv.shape[1] // 2), F32),
             pltpu.VMEM((4, depth, CORES * n), BF16),
             pltpu.VMEM((ROUNDS, rows, n), BF16),
             pltpu.VMEM((ROUNDS, 4, CORES, rows, n), F32),
@@ -454,17 +487,37 @@
     )(o, kv, x, w_out)
 
 
+def write_kernel(y_ref, k_ref, v_ref, y_out, k_out, v_out, sem):
+    lines = y_ref.shape[0] // WRITES
+    copies = [pltpu.make_async_copy(y_ref.at[pl.ds(i * lines, lines)], y_out.at[pl.ds(i * lines, lines)], sem.at[i])
+              for i in range(WRITES)]
+    copies.append(pltpu.make_async_copy(k_ref, k_out, sem.at[WRITES]))
+    copies.append(pltpu.make_async_copy(v_ref, v_out, sem.at[WRITES + 1]))
+    for copy in copies:
+        copy.start()
+    for copy in copies:
+        copy.wait()
+
+
+def write(*arrays):
+    return pl.pallas_call(
+        write_kernel,
+        out_shape=tuple(jax.ShapeDtypeStruct(a.shape, a.dtype) for a in arrays),
+        in_specs=[pl.BlockSpec(memory_space=pltpu.VMEM)] * 3,
+        out_specs=(pl.BlockSpec(memory_space=pltpu.HBM),) * 3,
+        scratch_shapes=[pltpu.SemaphoreType.DMA((WRITES + 2,))],
+        compiler_params=pltpu.CompilerParams(vmem_limit_bytes=1024 * 1024),
+        name="write",
+    )(*arrays)
+
+
 def solution(mesh):
     size = mesh.shape["model"]
 
     def local_step(x, w_query, w_key, w_value, w_out, k_cache, v_cache, lengths):
-        rows = x.shape[0]
-        head_dim = k_cache.shape[3]
-        kv_heads = k_cache.shape[1]
+        lengths = pltpu.with_memory_space_constraint(lengths, pltpu.HBM)
         out, kv = front(x, w_query, w_key, w_value, k_cache, v_cache, lengths)
-        y, kvs = out_product(size, out, kv, x, w_out)
-        kvs = kvs.reshape(rows, kv_heads, 2, head_dim)
-        return y, kvs[:, :, 0], kvs[:, :, 1]
+        return write(*out_product(size, out, kv, x, w_out))
 
     rows_spec = P("replica")
     return jax.shard_map(

time: 107 us -> 99.2 us (0.927)
  local copies, waits for them, and re-layouts: 4.62 us -> 0 us
  Pallas kernels: 101 us -> 97.8 us
    pallas_call x1, Pallas kernels: 36.3 us -> 30.6 us  [front(): pl.pallas_call(front_kernel, out_shape=(pltpu.VMEM((rows, width), BF16),...]
    unnamed x3 -> x0, local copies, waits for them, and re-layouts: 2.66 us -> none
    pallas_call x0 -> x1, Pallas kernels: none -> 2.25 us  [write(): pl.pallas_call(write_kernel, out_shape=tuple((jax.ShapeDtypeStruct(a.shap...]
where the time goes in v3:
time: 99.2 us; the launch traced here: 98.4 us
  Pallas kernels  97.8 us (99%)
    pallas_call x1, Pallas kernels, out_product(): pl.pallas_call(functools.partial(out_kernel, size), out_shape=(pltpu.VMEM...  65 us
    pallas_call x1, Pallas kernels, front(): pl.pallas_call(front_kernel, out_shape=(pltpu.VMEM((rows, width), BF16),...  30.6 us
    pallas_call x1, Pallas kernels, write(): pl.pallas_call(write_kernel, out_shape=tuple((jax.ShapeDtypeStruct(a.shap...  2.25 us

profile of v3, /device:TPU:113, one launch (start us, length us, event | category | flops | bytes accessed | tf_op | source)
XLA Modules:
  0.0 98.4 jit_solution(2609924517878425304)
XLA Ops:
  0.6 30.6 %front.1 = (bf16[128,2048]{1,0:T(8,128)(2,1)S(1)}, bf16[128,256]{1,0:T(8,128)(2,1)S(1)}) custom-call(bf16[128,16384]{1,0:T(8,128)(2,1)} %x_ref.3, bf16[16384,2048]{1,0:T(8,128)(2,1)} %wq_ref.1, bf16[16384,1024]{1,0:T(8,128)(2,1)} %wk_ref.1, bf16[16384,1024]{1,0:T(8,128)(2,1)} %wv_ref.1, bf16[128,8,256,128]{3,2,1,0:T(8,128)(2,1)} %kc_ref.1, ...), custom_call_target="tpu_custom_call" | custom-call | flops 9663676416 | bytes 75497472 | tf_op jit(solution)/shard_map/front/pallas_call | solution.py:201
  31.2 65.0 %out_reduce.1 = (bf16[128,16384]{1,0:T(8,128)(2,1)S(1)}, bf16[128,8,128]{2,1,0:T(8,128)(2,1)S(1)}, bf16[128,8,128]{2,1,0:T(8,128)(2,1)S(1)}) custom-call(bf16[128,2048]{1,0:T(8,128)(2,1)S(1)} %get-tuple-element.8.o_ref, bf16[128,256]{1,0:T(8,128)(2,1)S(1)} %get-tuple-element.9.kv_ref, bf16[128,16384]{1,0:T(8,128)(2,1)} %x_ref.3, bf16[2048,16384]{1,0:T(8,128)(2,1)} %w_ref.1), custom_call_target="tpu_custom_call" | custom-call | flops 8589934592 | bytes 67108864 | tf_op jit(solution)/shard_map/out_reduce/pallas_call | solution.py:456
  96.2 2.3 %write.1 = (bf16[128,16384]{1,0:T(8,128)(2,1)}, bf16[128,8,128]{2,1,0:T(8,128)(2,1)}, bf16[128,8,128]{2,1,0:T(8,128)(2,1)}) custom-call(bf16[128,16384]{1,0:T(8,128)(2,1)S(1)} %get-tuple-element.10.y_ref, bf16[128,8,128]{2,1,0:T(8,128)(2,1)S(1)} %get-tuple-element.11.k_ref, bf16[128,8,128]{2,1,0:T(8,128)(2,1)S(1)} %get-tuple-element.12.v_ref), custom_call_target="tpu_custom_call" | custom-call | tf_op jit(solution)/shard_map/write/pallas_call | solution.py:503

commit v4 on v3

--- a/solution.py
+++ b/solution.py
@@ -21,9 +21,9 @@
 F32 = jnp.float32
 
 
-def front_kernel(x_ref, wq_ref, wk_ref, wv_ref, kc_ref, vc_ref, len_ref, o_ref, kv_ref,
+def front_kernel(size, x_ref, wq_ref, wk_ref, wv_ref, kc_ref, vc_ref, wo_ref, len_ref, o_ref, kv_ref, first_ref,
                  xbuf, wbuf, acc, kvf, qbuf, obuf, kshort, vshort, klong, vlong, lens, order,
-                 x_sem, w_sem, short_sem, long_sem, len_sem):
+                 x_sem, w_sem, short_sem, long_sem, first_sem, len_sem):
     me = lax.axis_index("model")
     steps, rows, depth = xbuf.shape
     slots = wbuf.shape[0]
@@ -31,7 +31,6 @@
     width = heads * dim
     context = klong.shape[1]
     unit = context // SHORT
-    per_step = rows // steps
     head_cols = pl.ds(pl.multiple_of(me * dim, dim), dim)
 
     def x_copy(s):
@@ -67,10 +66,29 @@
     def _(s):
         x_copy(s).start()
 
+    def slab(j):
+        cols = slab_cols(size, j, OFFSETS[0], first_ref.shape[2] // CORES)
+        return pltpu.make_async_copy(wo_ref.at[:, cols], first_ref.at[j], first_sem.at[j])
+
     acc[...] = jnp.zeros_like(acc)
     len_copy.wait()
 
-    def stream(s, count):
+    def note(i, count):
+        for j in range(unit):
+            b = i * unit + j
+            is_long = lens[b] > SHORT - 1
+
+            @pl.when(is_long)
+            def _():
+                order[count] = b
+
+            count = count + is_long.astype(jnp.int32)
+        return count
+
+    count = lax.fori_loop(0, rows // unit, note, jnp.int32(0))
+
+    @pl.loop(0, steps)
+    def _(s):
         slot = lax.rem(s, slots)
         x_copy(s).wait()
         for copy in w_copies(s, slot):
@@ -82,31 +100,24 @@
             for copy in w_copies(s + slots, slot):
                 copy.start()
 
-        @pl.when(s == steps // 4)
+        @pl.when(s == steps - 2)
         def _():
             for copy in short_copies():
                 copy.start()
 
-        for i in range(per_step):
-            b = s * per_step + i
-            is_long = lens[b] > SHORT - 1
-
-            @pl.when(is_long)
-            def _():
-                order[count] = b
-                for copy in long_copies(b, count):
+            @pl.loop(0, count)
+            def _(i):
+                for copy in long_copies(order[i], i):
                     copy.start()
 
-            count = count + is_long.astype(jnp.int32)
-        return count
-
-    count = lax.fori_loop(0, steps, stream, jnp.int32(0))
+            for j in range(first_ref.shape[0]):
+                slab(j).start()
 
     kv = acc[:, width:].astype(BF16)
     kv_ref[...] = kv
     kvf[...] = kv.astype(F32)
     for h in range(heads):
-        qbuf[:, h, :] = acc[:, h * dim:(h + 1) * dim].astype(BF16).astype(F32)
+        qbuf[:, h, :] = acc[:, h * dim:(h + 1) * dim]
 
     inv_sqrt = dim ** -0.5
     contract_last = (((1,), (1,)), ((), ()))
@@ -188,9 +199,11 @@
 
     for h in range(heads):
         o_ref[:, h * dim:(h + 1) * dim] = obuf[:, h, :].astype(BF16)
-
-
-def front(x, w_query, w_key, w_value, k_cache, v_cache, lengths):
+    for j in range(first_ref.shape[0]):
+        slab(j).wait()
+
+
+def front(size, x, w_query, w_key, w_value, k_cache, v_cache, w_out, lengths):
     rows, model = x.shape
     width = w_query.shape[1]
     context, dim = k_cache.shape[2:]
@@ -198,11 +211,12 @@
     steps = model // DEPTH
     sem = pltpu.SemaphoreType.DMA
     total = width + 2 * dim
+    first = pltpu.VMEM((len(OFFSETS), width, model // (ROUNDS * size) * CORES), BF16)
     return pl.pallas_call(
-        front_kernel,
-        out_shape=(pltpu.VMEM((rows, width), BF16), pltpu.VMEM((rows, 2 * dim), BF16)),
-        in_specs=[pl.BlockSpec(memory_space=pl.ANY)] * 6 + [pl.BlockSpec(memory_space=pltpu.HBM)],
-        out_specs=(pl.BlockSpec(memory_space=pltpu.VMEM), pl.BlockSpec(memory_space=pltpu.VMEM)),
+        functools.partial(front_kernel, size),
+        out_shape=(pltpu.VMEM((rows, width), BF16), pltpu.VMEM((rows, 2 * dim), BF16), first),
+        in_specs=[pl.BlockSpec(memory_space=pl.ANY)] * 7 + [pl.BlockSpec(memory_space=pltpu.HBM)],
+        out_specs=(pl.BlockSpec(memory_space=pltpu.VMEM),) * 3,
         scratch_shapes=[
             pltpu.VMEM((steps, rows, DEPTH), BF16),
             pltpu.VMEM((4, DEPTH, total), BF16),
@@ -216,38 +230,41 @@
             pltpu.VMEM((rows, context, dim), BF16),
             pltpu.SMEM((rows,), jnp.int32),
             pltpu.SMEM((rows,), jnp.int32),
-            sem((steps,)), sem((4, 3)), sem((2,)), sem((2,)), sem,
+            sem((steps,)), sem((4, 3)), sem((2,)), sem((2,)), sem((len(OFFSETS),)), sem,
         ],
-        compiler_params=pltpu.CompilerParams(vmem_limit_bytes=52 * 1024 * 1024),
+        compiler_params=pltpu.CompilerParams(vmem_limit_bytes=48 * 1024 * 1024),
         cost_estimate=pl.CostEstimate(
             flops=2 * rows * model * total, bytes_accessed=model * total * 2, transcendentals=0),
         name="front",
-    )(x, w_query, w_key, w_value, k_cache, v_cache, lengths)
-
-
-def out_kernel(size, o_ref, kv_ref, x_ref, w_ref, y_ref, k_ref, v_ref,
+    )(x, w_query, w_key, w_value, k_cache, v_cache, w_out, lengths)
+
+
+def slab_cols(size, r, offset, n):
+    chips = size // CORES
+    dest = lax.rem(lax.axis_index("model") // CORES + offset, chips)
+    return pl.ds(pl.multiple_of((r * chips + dest) * (CORES * n), CORES * n), CORES * n)
+
+
+def out_kernel(size, o_ref, kv_ref, first_ref, x_ref, w_ref, y_ref, k_ref, v_ref,
                kvs_ref, kv_heads, wbuf, xbuf, part, pair, hop, near,
                w_sem, x_sem, kv_sem, pair_send, pair_recv, hop_send, hop_recv, near_send, near_recv,
                ag_send, ag_recv, fwd_send, fwd_recv):
     me = lax.axis_index("model")
     core = lax.rem(me, CORES)
-    chip = me // CORES
-    chips = size // CORES
     plus = lax.rem(me + CORES, size)
     minus = lax.rem(me + size - CORES, size)
     mate = me + 1 - 2 * core
     plus2 = lax.rem(me + 2 * CORES, size)
     rows, depth = o_ref.shape
     half = rows // 2
+    slots = wbuf.shape[0]
     n, nk = part.shape[-1], kv_ref.shape[1]
     width = n * size
     top, bottom = pl.ds(0, half), pl.ds(half, half)
     kv_round = ROUNDS
 
-    def slab(r, j):
-        dest = lax.rem(chip + OFFSETS[j], chips)
-        cols = pl.ds(pl.multiple_of(r * width + dest * (CORES * n), CORES * n), CORES * n)
-        return pltpu.make_async_copy(w_ref.at[:, cols], wbuf.at[j], w_sem.at[j])
+    def slab(r, offset, slot):
+        return pltpu.make_async_copy(w_ref.at[:, slab_cols(size, r, offset, n)], wbuf.at[slot], w_sem.at[slot])
 
     def own_x(r):
         cols = pl.ds(pl.multiple_of(r * width + me * n, n), n)
@@ -265,12 +282,9 @@
         to, lines = ((plus, top), (minus, bottom))[way]
         return remote(part.at[r, 0, core, lines], hop.at[r, way], hop_send.at[r, way], hop_recv.at[r, way], to)
 
-    def near_copy(r, way, late):
-        to = (plus, minus)[way]
-        lines = top if (way == 0) == late else bottom
-        k = 2 * way + int(late)
-        return remote(part.at[r, 1 + way, core, lines], near.at[r, way, lines],
-                      near_send.at[r, k], near_recv.at[r, k], to)
+    def near_copy(r, way):
+        return remote(part.at[r, 1 + way, core], near.at[r, way], near_send.at[r, way], near_recv.at[r, way],
+                      (plus, minus)[way])
 
     def block(r, owner, lines):
         if r is None:
@@ -312,8 +326,8 @@
         ref = block(r, owner + flip, lines)
         return remote(ref, ref, fwd_send.at[i, k], fwd_recv.at[i, k], mate)
 
-    for j in range(4):
-        slab(0, j).start()
+    for slot in range(slots):
+        slab(slots + slot, OFFSETS[0], slot).start()
     own_kv = pltpu.make_async_copy(kv_ref, kvs_ref.at[:, pl.ds(pl.multiple_of(me * nk, nk), nk)], kv_sem)
     own_kv.start()
 
@@ -333,18 +347,18 @@
     def pair_sum(r, j):
         pair_copy(r, j).wait_recv()
         part[r, j, core] = part[r, j, core] + pair[r, j]
-        if j == 0:
-            for way in range(2):
-                hop_copy(r, way).start()
-        elif j < 3:
-            near_copy(r, j - 1, False).start()
-
-    def add_hops(r):
-        for way in range(2):
-            hop_copy(r, way).wait_recv()
-            lines = (top, bottom)[way]
-            part[r, 1 + way, core, lines] = part[r, 1 + way, core, lines] + hop[r, way]
-            near_copy(r, way, True).start()
+
+    def send_hops(r):
+        pair_sum(r, 0)
+        for way in range(2):
+            hop_copy(r, way).start()
+
+    def send_near(r, way):
+        pair_sum(r, 1 + way)
+        hop_copy(r, way).wait_recv()
+        lines = (top, bottom)[way]
+        part[r, 1 + way, core, lines] = part[r, 1 + way, core, lines] + hop[r, way]
+        near_copy(r, way).start()
 
     def relay(r):
         for way in range(2):
@@ -357,42 +371,76 @@
             relayed_recv(r, way).wait_recv()
             fwd_copy(r, 2 + way).start()
 
-    @pl.loop(0, ROUNDS)
-    def _(r):
-        for j in range(4):
-            slab(r, j).wait()
-            product = jnp.dot(o_ref[...], wbuf[j], preferred_element_type=F32)
-            for q in range(CORES):
-                part[r, j, q] = product[:, q * n:(q + 1) * n]
-            pair_copy(r, j).start()
-
-            @pl.when(r < ROUNDS - 1)
-            def _():
-                slab(r + 1, j).start()
-
-            if j >= 2:
-                pair_sum(r, j - 2)
-            else:
-                @pl.when(r >= 1)
-                def _():
-                    pair_sum(r - 1, j + 2)
-
-        @pl.when(r == 0)
-        def _():
-            relay(None)
-
-        @pl.when(r == 2)
-        def _():
-            pass_far(None)
+    def multiply(r, j, weights):
+        product = jnp.dot(o_ref[...], weights[...], preferred_element_type=F32)
+        for q in range(CORES):
+            part[r, j, q] = product[:, q * n:(q + 1) * n]
+        pair_copy(r, j).start()
+
+    @pl.loop(0, slots)
+    def _(r):
+        multiply(r, 0, first_ref.at[r])
 
         @pl.when(r >= 2)
         def _():
-            add_hops(r - 2)
-
-    for j in (2, 3):
-        pair_sum(ROUNDS - 1, j)
+            send_hops(r - 2)
+
+    @pl.loop(slots, ROUNDS)
+    def _(r):
+        slot = r - slots
+        slab(r, OFFSETS[0], slot).wait()
+        multiply(r, 0, wbuf.at[slot])
+        slab(slot // 2, OFFSETS[1] + 2 * lax.rem(slot, 2), slot).start()
+        send_hops(r - 2)
+
+    relay(None)
+
+    @pl.loop(0, ROUNDS)
+    def _(r):
+        for way in range(2):
+            slot = 2 * lax.rem(r, 2) + way
+            slab(r, OFFSETS[1 + way], slot).wait()
+            multiply(r, 1 + way, wbuf.at[slot])
+
+            @pl.when(r < ROUNDS - 2)
+            def _():
+                slab(r + 2, OFFSETS[1 + way], slot).start()
+
+            @pl.when(r >= ROUNDS - 2)
+            def _():
+                slab(2 * (r - (ROUNDS - 2)) + way, OFFSETS[3], slot).start()
+
+            @pl.when(r == 0)
+            def _():
+                send_hops(ROUNDS - 2 + way)
+
+            @pl.when(r >= 1)
+            def _():
+                send_near(r - 1, way)
+
+    pass_far(None)
+
+    @pl.loop(0, ROUNDS)
+    def _(r):
+        slot = lax.rem(r, slots)
+        slab(r, OFFSETS[3], slot).wait()
+        multiply(r, 3, wbuf.at[slot])
+
+        @pl.when(r < ROUNDS - slots)
+        def _():
+            slab(r + slots, OFFSETS[3], slot).start()
+
+        for way in range(2):
+            @pl.when(r == way)
+            def _():
+                send_near(ROUNDS - 1, way)
+
+        @pl.when(r >= 2)
+        def _():
+            pair_sum(r - 2, 3)
+
     for r in (ROUNDS - 2, ROUNDS - 1):
-        add_hops(r)
+        pair_sum(r, 3)
 
     def drain(r):
         received(r, 0).wait_recv()
@@ -414,8 +462,7 @@
 
     def finish(r):
         for way in range(2):
-            for late in (False, True):
-                near_copy(r, way, late).wait_recv()
+            near_copy(r, way).wait_recv()
         own_x(r).wait()
         total = part[r, 3, core] + (near[r, 0] + near[r, 1])
         total = xbuf[r].astype(F32) + total
@@ -423,19 +470,17 @@
         for k in range(3):
             gather_copy(r, k).start()
 
-    @pl.loop(0, ROUNDS + 4)
-    def _(i):
-        @pl.when(i < ROUNDS)
-        def _():
-            finish(i)
-
-        @pl.when((i >= 2) & (i < ROUNDS + 2))
-        def _():
-            relay(i - 2)
-
-        @pl.when(i >= 4)
-        def _():
-            pass_far(i - 4)
+    @pl.loop(0, ROUNDS)
+    def _(r):
+        finish(r)
+
+    @pl.loop(0, ROUNDS)
+    def _(r):
+        relay(r)
+
+    @pl.loop(0, ROUNDS)
+    def _(r):
+        pass_far(r)
 
     @pl.loop(0, ROUNDS)
     def _(r):
@@ -443,12 +488,11 @@
             pair_copy(r, j).wait_send()
         for way in range(2):
             hop_copy(r, way).wait_send()
-            for late in (False, True):
-                near_copy(r, way, late).wait_send()
+            near_copy(r, way).wait_send()
         drain(r)
 
 
-def out_product(size, o, kv, x, w_out):
+def out_product(size, o, kv, first, x, w_out):
     rows, depth = o.shape
     model = w_out.shape[1]
     n = model // (ROUNDS * size)
@@ -459,6 +503,7 @@
         in_specs=[
             pl.BlockSpec(memory_space=pltpu.VMEM),
             pl.BlockSpec(memory_space=pl.ANY),
+            pl.BlockSpec(memory_space=pltpu.VMEM),
             pl.BlockSpec(memory_space=pl.ANY),
             pl.BlockSpec(memory_space=pl.ANY),
         ],
@@ -475,16 +520,16 @@
             sem((4,)), sem((ROUNDS,)), sem,
             sem((ROUNDS, 4)), sem((ROUNDS, 4)),
             sem((ROUNDS, 2)), sem((ROUNDS, 2)),
-            sem((ROUNDS, 4)), sem((ROUNDS, 4)),
+            sem((ROUNDS, 2)), sem((ROUNDS, 2)),
             sem((ROUNDS + 1, 5)), sem((ROUNDS + 1, 5)),
             sem((ROUNDS + 1, 4)), sem((ROUNDS + 1, 4)),
         ],
         compiler_params=pltpu.CompilerParams(
-            collective_id=0, has_side_effects=True, vmem_limit_bytes=48 * 1024 * 1024),
+            collective_id=0, has_side_effects=True, vmem_limit_bytes=36 * 1024 * 1024),
         cost_estimate=pl.CostEstimate(
             flops=2 * rows * depth * model, bytes_accessed=depth * model * 2, transcendentals=0),
         name="out_reduce",
-    )(o, kv, x, w_out)
+    )(o, kv, first, x, w_out)
 
 
 def write_kernel(y_ref, k_ref, v_ref, y_out, k_out, v_out, sem):
@@ -515,9 +560,10 @@
     size = mesh.shape["model"]
 
     def local_step(x, w_query, w_key, w_value, w_out, k_cache, v_cache, lengths):
+        x = pltpu.with_memory_space_constraint(x, pltpu.HBM)
         lengths = pltpu.with_memory_space_constraint(lengths, pltpu.HBM)
-        out, kv = front(x, w_query, w_key, w_value, k_cache, v_cache, lengths)
-        return write(*out_product(size, out, kv, x, w_out))
+        out, kv, first = front(size, x, w_query, w_key, w_value, k_cache, v_cache, w_out, lengths)
+        return write(*out_product(size, out, kv, first, x, w_out))
 
     rows_spec = P("replica")
     return jax.shard_map(

time: 99.2 us -> 96.3 us (0.971)
  Pallas kernels: 97.8 us -> 95.5 us
    pallas_call x1, Pallas kernels: 65 us -> 62.8 us  [out_product(): pl.pallas_call(functools.partial(out_kernel, size), out_shape=(pltpu.VMEM...]
where the time goes in v4:
time: 96.3 us; the launch traced here: 96.1 us
  Pallas kernels  95.5 us (99%)
    pallas_call x1, Pallas kernels, out_product(): pl.pallas_call(functools.partial(out_kernel, size), out_shape=(pltpu.VMEM...  62.8 us
    pallas_call x1, Pallas kernels, front(): pl.pallas_call(functools.partial(front_kernel, size), out_shape=(pltpu.VM...  30.5 us
    pallas_call x1, Pallas kernels, write(): pl.pallas_call(write_kernel, out_shape=tuple((jax.ShapeDtypeStruct(a.shap...  2.25 us

profile of v4, /device:TPU:113, one launch (start us, length us, event | category | flops | bytes accessed | tf_op | source)
XLA Modules:
  0.0 96.1 jit_solution(7672181417693060198)
XLA Ops:
  0.6 30.5 %front.1 = (bf16[128,2048]{1,0:T(8,128)(2,1)S(1)}, bf16[128,256]{1,0:T(8,128)(2,1)S(1)}, bf16[4,2048,512]{2,1,0:T(8,128)(2,1)S(1)}) custom-call(bf16[128,16384]{1,0:T(8,128)(2,1)} %x_ref.3, bf16[16384,2048]{1,0:T(8,128)(2,1)} %wq_ref.1, bf16[16384,1024]{1,0:T(8,128)(2,1)} %wk_ref.1, bf16[16384,1024]{1,0:T(8,128)(2,1)} %wv_ref.1, ...), custom_call_target="tpu_custom_call" | custom-call | flops 9663676416 | bytes 75497472 | tf_op jit(solution)/shard_map/front/pallas_call | solution.py:215
  31.1 62.8 %out_reduce.1 = (bf16[128,16384]{1,0:T(8,128)(2,1)S(1)}, bf16[128,8,128]{2,1,0:T(8,128)(2,1)S(1)}, bf16[128,8,128]{2,1,0:T(8,128)(2,1)S(1)}) custom-call(bf16[128,2048]{1,0:T(8,128)(2,1)S(1)} %get-tuple-element.9.o_ref, bf16[128,256]{1,0:T(8,128)(2,1)S(1)} %get-tuple-element.10.kv_ref, bf16[4,2048,512]{2,1,0:T(8,128)(2,1)S(1)} %get-tuple-element.11.first_ref, ...), custom_call_target="tpu_custom_call" | custom-call | flops 8589934592 | bytes 67108864 | tf_op jit(solution)/shard_map/out_reduce/pallas_call | solution.py:500
  93.9 2.3 %write.1 = (bf16[128,16384]{1,0:T(8,128)(2,1)}, bf16[128,8,128]{2,1,0:T(8,128)(2,1)}, bf16[128,8,128]{2,1,0:T(8,128)(2,1)}) custom-call(bf16[128,16384]{1,0:T(8,128)(2,1)S(1)} %get-tuple-element.12.y_ref, bf16[128,8,128]{2,1,0:T(8,128)(2,1)S(1)} %get-tuple-element.13.k_ref, bf16[128,8,128]{2,1,0:T(8,128)(2,1)S(1)} %get-tuple-element.14.v_ref), custom_call_target="tpu_custom_call" | custom-call | tf_op jit(solution)/shard_map/write/pallas_call | solution.py:548

commit v5 on v4

--- a/solution.py
+++ b/solution.py
@@ -27,7 +27,8 @@
     me = lax.axis_index("model")
     steps, rows, depth = xbuf.shape
     slots = wbuf.shape[0]
-    heads, dim = qbuf.shape[1:]
+    dim = qbuf.shape[1]
+    heads = qbuf.shape[0] // rows
     width = heads * dim
     context = klong.shape[1]
     unit = context // SHORT
@@ -35,15 +36,13 @@
 
     def x_copy(s):
         cols = pl.ds(pl.multiple_of(s * depth, depth), depth)
-        return pltpu.make_async_copy(x_ref.at[:, cols], xbuf.at[s], x_sem.at[s])
+        return pltpu.make_async_copy(x_ref.at[:, cols], xbuf.at[s], x_sem.at[lax.rem(s, slots)])
 
     def w_copies(s, slot):
         lines = pl.ds(pl.multiple_of(s * depth, depth), depth)
-        return (
-            pltpu.make_async_copy(wq_ref.at[lines], wbuf.at[slot, :, pl.ds(0, width)], w_sem.at[slot, 0]),
-            pltpu.make_async_copy(wk_ref.at[lines, head_cols], wbuf.at[slot, :, pl.ds(width, dim)], w_sem.at[slot, 1]),
-            pltpu.make_async_copy(wv_ref.at[lines, head_cols], wbuf.at[slot, :, pl.ds(width + dim, dim)], w_sem.at[slot, 2]),
-        )
+        return [pltpu.make_async_copy(src, wbuf.at[slot, :, pl.ds(at, size)], w_sem.at[slot]) for src, at, size in (
+            (wq_ref.at[lines], 0, width), (wk_ref.at[lines, head_cols], width, dim),
+            (wv_ref.at[lines, head_cols], width + dim, dim))]
 
     def short_copies():
         lines = pl.ds(0, SHORT)
@@ -62,13 +61,9 @@
         if s == 0:
             len_copy.start()
 
-    @pl.loop(slots, steps)
-    def _(s):
-        x_copy(s).start()
-
     def slab(j):
         cols = slab_cols(size, j, OFFSETS[0], first_ref.shape[2] // CORES)
-        return pltpu.make_async_copy(wo_ref.at[:, cols], first_ref.at[j], first_sem.at[j])
+        return pltpu.make_async_copy(wo_ref.at[:, cols], first_ref.at[j], first_sem)
 
     acc[...] = jnp.zeros_like(acc)
     len_copy.wait()
@@ -91,12 +86,12 @@
     def _(s):
         slot = lax.rem(s, slots)
         x_copy(s).wait()
-        for copy in w_copies(s, slot):
-            copy.wait()
+        pltpu.make_async_copy(wbuf.at[slot], wbuf.at[slot], w_sem.at[slot]).wait()
         acc[...] += jnp.dot(xbuf[s], wbuf[slot], preferred_element_type=F32)
 
         @pl.when(s + slots < steps)
         def _():
+            x_copy(s + slots).start()
             for copy in w_copies(s + slots, slot):
                 copy.start()
 
@@ -117,7 +112,7 @@
     kv_ref[...] = kv
     kvf[...] = kv.astype(F32)
     for h in range(heads):
-        qbuf[:, h, :] = acc[:, h * dim:(h + 1) * dim]
+        qbuf[pl.ds(h, rows, stride=heads), :] = acc[:, h * dim:(h + 1) * dim]
 
     inv_sqrt = dim ** -0.5
     contract_last = (((1,), (1,)), ((), ()))
@@ -169,12 +164,13 @@
             for j in range(unit):
                 bound = jnp.where(line // SHORT == j, lens[first + j], bound)
             seqs = pl.ds(pl.multiple_of(first, unit), unit)
-            places.append(seqs)
+            lines = pl.ds(pl.multiple_of(first * heads, short_rows), short_rows)
+            places.append(lines)
             items.append((
-                qbuf[seqs].reshape(short_rows, dim).astype(BF16),
+                qbuf[lines].astype(BF16),
                 kshort[seqs].reshape(context, dim), vshort[seqs].reshape(context, dim), place < bound))
-        for seqs, out in zip(places, attend(items)):
-            obuf[seqs] = out.reshape(unit, heads, dim)
+        for lines, out in zip(places, attend(items)):
+            obuf[lines] = out
 
     @pl.loop(0, count)
     def _(i):
@@ -192,15 +188,15 @@
     def _(i):
         slots = [jnp.minimum(i * LONG_STEP + j, count - 1) for j in range(LONG_STEP)]
         seqs = [order[slot] for slot in slots]
-        outs = attend([(qbuf[b].astype(BF16), klong[slot], vlong[slot], long_place < lens[b])
-                       for slot, b in zip(slots, seqs)])
-        for b, out in zip(seqs, outs):
-            obuf[b] = out
+        lines = [pl.ds(pl.multiple_of(b * heads, heads), heads) for b in seqs]
+        outs = attend([(qbuf[here].astype(BF16), klong[slot], vlong[slot], long_place < lens[b])
+                       for here, slot, b in zip(lines, slots, seqs)])
+        for here, out in zip(lines, outs):
+            obuf[here] = out
 
     for h in range(heads):
-        o_ref[:, h * dim:(h + 1) * dim] = obuf[:, h, :].astype(BF16)
-    for j in range(first_ref.shape[0]):
-        slab(j).wait()
+        o_ref[:, h * dim:(h + 1) * dim] = obuf[pl.ds(h, rows, stride=heads), :].astype(BF16)
+    pltpu.make_async_copy(first_ref, first_ref, first_sem).wait()
 
 
 def front(size, x, w_query, w_key, w_value, k_cache, v_cache, w_out, lengths):
@@ -222,15 +218,15 @@
             pltpu.VMEM((4, DEPTH, total), BF16),
             pltpu.VMEM((rows, total), F32),
             pltpu.VMEM((rows, 2 * dim), F32),
-            pltpu.VMEM((rows, heads, dim), F32),
-            pltpu.VMEM((rows, heads, dim), F32),
+            pltpu.VMEM((rows * heads, dim), F32),
+            pltpu.VMEM((rows * heads, dim), F32),
             pltpu.VMEM((rows, SHORT, dim), BF16),
             pltpu.VMEM((rows, SHORT, dim), BF16),
             pltpu.VMEM((rows, context, dim), BF16),
             pltpu.VMEM((rows, context, dim), BF16),
             pltpu.SMEM((rows,), jnp.int32),
             pltpu.SMEM((rows,), jnp.int32),
-            sem((steps,)), sem((4, 3)), sem((2,)), sem((2,)), sem((len(OFFSETS),)), sem,
+            sem((4,)), sem((4,)), sem((2,)), sem((2,)), sem, sem,
         ],
         compiler_params=pltpu.CompilerParams(vmem_limit_bytes=48 * 1024 * 1024),
         cost_estimate=pl.CostEstimate(
@@ -247,8 +243,7 @@
 
 def out_kernel(size, o_ref, kv_ref, first_ref, x_ref, w_ref, y_ref, k_ref, v_ref,
                kvs_ref, kv_heads, wbuf, xbuf, part, pair, hop, near,
-               w_sem, x_sem, kv_sem, pair_send, pair_recv, hop_send, hop_recv, near_send, near_recv,
-               ag_send, ag_recv, fwd_send, fwd_recv):
+               w_sem, x_sem, kv_sem, sent, pair_recv, hop_recv, near_recv, ag_recv, relay_recv, mate_recv):
     me = lax.axis_index("model")
     core = lax.rem(me, CORES)
     plus = lax.rem(me + CORES, size)
@@ -268,63 +263,69 @@
 
     def own_x(r):
         cols = pl.ds(pl.multiple_of(r * width + me * n, n), n)
-        return pltpu.make_async_copy(x_ref.at[:, cols], xbuf.at[r], x_sem.at[r])
+        return pltpu.make_async_copy(x_ref.at[:, cols], xbuf.at[r], x_sem)
 
     def remote(src, dst, send, recv, to):
         return pltpu.make_async_remote_copy(
             src_ref=src, dst_ref=dst, send_sem=send, recv_sem=recv,
             device_id={"model": to}, device_id_type=MESH)
 
+    PAIR, HOP, NEAR, GATHER, FORWARD = range(5)
+
     def pair_copy(r, j):
-        return remote(part.at[r, j, 1 - core], pair.at[r, j], pair_send.at[r, j], pair_recv.at[r, j], mate)
+        recv = pair_recv.at[(len(OFFSETS) - 1) * ROUNDS if j == len(OFFSETS) - 1 else j * ROUNDS + r]
+        return remote(part.at[r, j, 1 - core], pair.at[r, j], sent.at[PAIR], recv, mate)
 
     def hop_copy(r, way):
         to, lines = ((plus, top), (minus, bottom))[way]
-        return remote(part.at[r, 0, core, lines], hop.at[r, way], hop_send.at[r, way], hop_recv.at[r, way], to)
+        return remote(part.at[r, 0, core, lines], hop.at[r, way], sent.at[HOP], hop_recv.at[r], to)
 
     def near_copy(r, way):
-        return remote(part.at[r, 1 + way, core], near.at[r, way], near_send.at[r, way], near_recv.at[r, way],
-                      (plus, minus)[way])
+        return remote(part.at[r, 1 + way, core], near.at[r, way], sent.at[NEAR], near_recv.at[r], (plus, minus)[way])
 
     def block(r, owner, lines):
         if r is None:
             return kvs_ref.at[lines, pl.ds(pl.multiple_of(owner * nk, nk), nk)]
         return y_ref.at[lines, pl.ds(pl.multiple_of(r * width + owner * n, n), n)]
 
+    def blocks(r, count):
+        if r is None:
+            return kvs_ref.at[:, pl.ds(0, count * nk)]
+        return y_ref.at[:, pl.ds(0, count * n)]
+
     everything = pl.ds(0, rows)
 
-    def gather_copy(r, k):
-        i = kv_round if r is None else r
+    def sems(r):
+        i, kind = (ROUNDS, 1) if r is None else (r, 0)
+        return sent.at[GATHER + 2 * kind], sent.at[FORWARD + 2 * kind], ag_recv.at[i], relay_recv.at[i], mate_recv.at[kind]
+
+    def wait_for(ref, sem):
+        remote(ref, ref, sem, sem, mate).wait_recv()
+
+    def gather(r):
+        send, _, recv, _, mate_sem = sems(r)
         ref = block(r, me, everything)
-        return remote(ref, ref, ag_send.at[i, k], ag_recv.at[i, k], (mate, plus, minus)[k])
-
-    def relay_copy(r, way):
-        i = kv_round if r is None else r
-        ref = block(r, (minus, plus)[way], (top, bottom)[way])
-        return remote(ref, ref, ag_send.at[i, 3 + way], ag_recv.at[i, 3 + way], (plus, minus)[way])
-
-    def relayed_recv(r, way):
-        i = kv_round if r is None else r
-        ref = block(r, plus2, (top, bottom)[way])
-        return remote(ref, ref, ag_send.at[i, 3 + way], ag_recv.at[i, 3 + way], (plus, minus)[way])
-
-    def received(r, k):
-        i = kv_round if r is None else r
-        ref = block(r, (mate, minus, plus)[k], everything)
-        return remote(ref, ref, ag_send.at[i, k], ag_recv.at[i, k], (mate, plus, minus)[k])
-
-    def fwd_copy(r, k):
-        i = kv_round if r is None else r
-        owner, lines = ((minus, everything), (plus, everything), (plus2, top), (plus2, bottom))[k]
+        for to, sem in ((plus, recv), (minus, recv), (mate, mate_sem)):
+            remote(ref, ref, send, sem, to).start()
+
+    def forward(r, owner, lines):
+        _, send, _, _, sem = sems(r)
         ref = block(r, owner, lines)
-        return remote(ref, ref, fwd_send.at[i, k], fwd_recv.at[i, k], mate)
-
-    def fwd_recv_copy(r, k):
-        i = kv_round if r is None else r
-        flip = 1 - 2 * core
-        owner, lines = ((minus, everything), (plus, everything), (plus2, top), (plus2, bottom))[k]
-        ref = block(r, owner + flip, lines)
-        return remote(ref, ref, fwd_send.at[i, k], fwd_recv.at[i, k], mate)
+        remote(ref, ref, send, sem, mate).start()
+
+    def relay(r):
+        send, _, recv, relay_sem, _ = sems(r)
+        wait_for(blocks(r, 2), recv)
+        for owner, lines, to in ((minus, top, plus), (plus, bottom, minus)):
+            ref = block(r, owner, lines)
+            remote(ref, ref, send, relay_sem, to).start()
+        for owner in (minus, plus):
+            forward(r, owner, everything)
+
+    def pass_far(r):
+        _, _, _, sem, _ = sems(r)
+        wait_for(blocks(r, 1), sem)
+        forward(r, plus2, everything)
 
     for slot in range(slots):
         slab(slots + slot, OFFSETS[0], slot).start()
@@ -341,8 +342,7 @@
 
     own_kv.wait()
     pl.semaphore_wait(barrier, 3)
-    for k in range(3):
-        gather_copy(None, k).start()
+    gather(None)
 
     def pair_sum(r, j):
         pair_copy(r, j).wait_recv()
@@ -355,21 +355,11 @@
 
     def send_near(r, way):
         pair_sum(r, 1 + way)
-        hop_copy(r, way).wait_recv()
+        if way == 0:
+            wait_for(hop.at[r], hop_recv.at[r])
         lines = (top, bottom)[way]
         part[r, 1 + way, core, lines] = part[r, 1 + way, core, lines] + hop[r, way]
         near_copy(r, way).start()
-
-    def relay(r):
-        for way in range(2):
-            received(r, 1 + way).wait_recv()
-            relay_copy(r, way).start()
-            fwd_copy(r, way).start()
-
-    def pass_far(r):
-        for way in range(2):
-            relayed_recv(r, way).wait_recv()
-            fwd_copy(r, 2 + way).start()
 
     def multiply(r, j, weights):
         product = jnp.dot(o_ref[...], weights[...], preferred_element_type=F32)
@@ -435,61 +425,36 @@
             def _():
                 send_near(ROUNDS - 1, way)
 
-        @pl.when(r >= 2)
-        def _():
-            pair_sum(r - 2, 3)
-
-    for r in (ROUNDS - 2, ROUNDS - 1):
-        pair_sum(r, 3)
-
-    def drain(r):
-        received(r, 0).wait_recv()
-        for k in range(4):
-            fwd_recv_copy(r, k).wait_recv()
-        for k in range(3):
-            gather_copy(r, k).wait_send()
-        for way in range(2):
-            relay_copy(r, way).wait_send()
-        for k in range(4):
-            fwd_copy(r, k).wait_send()
-
-    drain(None)
+    wait_for(blocks(None, 4), mate_recv.at[1])
     dim = nk // 2
     for i, ref in enumerate((k_ref, v_ref)):
         for owner in range(size):
-            kv_heads[:, owner, :] = kvs_ref[:, owner * nk + i * dim:owner * nk + (i + 1) * dim].astype(F32)
-        ref[...] = kv_heads[...].astype(BF16)
-
-    def finish(r):
-        for way in range(2):
-            near_copy(r, way).wait_recv()
-        own_x(r).wait()
-        total = part[r, 3, core] + (near[r, 0] + near[r, 1])
+            kv_heads[pl.ds(owner, rows, stride=size), :] = kvs_ref[:, owner * nk + i * dim:owner * nk + (i + 1) * dim].astype(F32)
+        ref[...] = kv_heads[...].astype(BF16).reshape(ref.shape)
+
+    wait_for(pair.at[:, 3], pair_recv.at[3 * ROUNDS])
+    pltpu.make_async_copy(xbuf, xbuf, x_sem).wait()
+
+    @pl.loop(0, ROUNDS)
+    def _(r):
+        wait_for(near.at[r], near_recv.at[r])
+        total = (part[r, 3, core] + pair[r, 3]) + (near[r, 0] + near[r, 1])
         total = xbuf[r].astype(F32) + total
         y_ref[:, pl.ds(pl.multiple_of(r * width + me * n, n), n)] = total.astype(BF16)
-        for k in range(3):
-            gather_copy(r, k).start()
+        gather(r)
 
     @pl.loop(0, ROUNDS)
     def _(r):
-        finish(r)
+        relay(r)
 
     @pl.loop(0, ROUNDS)
     def _(r):
-        relay(r)
-
-    @pl.loop(0, ROUNDS)
-    def _(r):
         pass_far(r)
 
-    @pl.loop(0, ROUNDS)
-    def _(r):
-        for j in range(4):
-            pair_copy(r, j).wait_send()
-        for way in range(2):
-            hop_copy(r, way).wait_send()
-            near_copy(r, way).wait_send()
-        drain(r)
+    wait_for(blocks(0, 4 * ROUNDS), mate_recv.at[0])
+    for ref, kind in ((pair, PAIR), (hop, HOP), (near, NEAR), (blocks(0, 4 * ROUNDS), GATHER), (blocks(0, 3 * ROUNDS), FORWARD),
+                      (blocks(None, 4), GATHER + 2), (blocks(None, 3), FORWARD + 2)):
+        wait_for(ref, sent.at[kind])
 
 
 def out_product(size, o, kv, first, x, w_out):
@@ -510,19 +475,15 @@
         out_specs=(pl.BlockSpec(memory_space=pltpu.VMEM),) * 3,
         scratch_shapes=[
             pltpu.VMEM((rows, size * kv.shape[1]), BF16),
-            pltpu.VMEM((rows, size, kv.shape[1] // 2), F32),
+            pltpu.VMEM((rows * size, kv.shape[1] // 2), F32),
             pltpu.VMEM((4, depth, CORES * n), BF16),
             pltpu.VMEM((ROUNDS, rows, n), BF16),
             pltpu.VMEM((ROUNDS, 4, CORES, rows, n), F32),
             pltpu.VMEM((ROUNDS, 4, rows, n), F32),
             pltpu.VMEM((ROUNDS, 2, rows // 2, n), F32),
             pltpu.VMEM((ROUNDS, 2, rows, n), F32),
-            sem((4,)), sem((ROUNDS,)), sem,
-            sem((ROUNDS, 4)), sem((ROUNDS, 4)),
-            sem((ROUNDS, 2)), sem((ROUNDS, 2)),
-            sem((ROUNDS, 2)), sem((ROUNDS, 2)),
-            sem((ROUNDS + 1, 5)), sem((ROUNDS + 1, 5)),
-            sem((ROUNDS + 1, 4)), sem((ROUNDS + 1, 4)),
+            sem((4,)), sem, sem, sem((7,)),
+            sem((3 * ROUNDS + 1,)), sem((ROUNDS,)), sem((ROUNDS,)), sem((ROUNDS + 1,)), sem((ROUNDS + 1,)), sem((2,)),
         ],
         compiler_params=pltpu.CompilerParams(
             collective_id=0, has_side_effects=True, vmem_limit_bytes=36 * 1024 * 1024),

time: 96.3 us -> 93.5 us (0.971)
  Pallas kernels: 95.5 us -> 92.8 us
    pallas_call x1, Pallas kernels: 62.8 us -> 60.8 us  [out_product(): pl.pallas_call(functools.partial(out_kernel, size), out_shape=(pltpu.VMEM...]
where the time goes in v5:
time: 93.5 us
  Pallas kernels  92.8 us (99%)
    pallas_call x1, Pallas kernels, out_product(): pl.pallas_call(functools.partial(out_kernel, size), out_shape=(pltpu.VMEM...  60.8 us
    pallas_call x1, Pallas kernels, front(): pl.pallas_call(functools.partial(front_kernel, size), out_shape=(pltpu.VM...  29.8 us
    pallas_call x1, Pallas kernels, write(): pl.pallas_call(write_kernel, out_shape=tuple((jax.ShapeDtypeStruct(a.shap...  2.25 us

profile of v5, /device:TPU:113, one launch (start us, length us, event | category | flops | bytes accessed | tf_op | source)
XLA Modules:
  0.0 93.5 jit_solution(12392855339275471734)
XLA Ops:
  0.6 29.8 %front.1 = (bf16[128,2048]{1,0:T(8,128)(2,1)S(1)}, bf16[128,256]{1,0:T(8,128)(2,1)S(1)}, bf16[4,2048,512]{2,1,0:T(8,128)(2,1)S(1)}) custom-call(bf16[128,16384]{1,0:T(8,128)(2,1)} %x_ref.3, bf16[16384,2048]{1,0:T(8,128)(2,1)} %wq_ref.1, bf16[16384,1024]{1,0:T(8,128)(2,1)} %wk_ref.1, bf16[16384,1024]{1,0:T(8,128)(2,1)} %wv_ref.1, ...), custom_call_target="tpu_custom_call" | custom-call | flops 9663676416 | bytes 75497472 | tf_op jit(solution)/shard_map/front/pallas_call | solution.py:211
  30.4 60.8 %out_reduce.1 = (bf16[128,16384]{1,0:T(8,128)(2,1)S(1)}, bf16[128,8,128]{2,1,0:T(8,128)(2,1)S(1)}, bf16[128,8,128]{2,1,0:T(8,128)(2,1)S(1)}) custom-call(bf16[128,2048]{1,0:T(8,128)(2,1)S(1)} %get-tuple-element.9.o_ref, bf16[128,256]{1,0:T(8,128)(2,1)S(1)} %get-tuple-element.10.kv_ref, bf16[4,2048,512]{2,1,0:T(8,128)(2,1)S(1)} %get-tuple-element.11.first_ref, ...), custom_call_target="tpu_custom_call" | custom-call | flops 8589934592 | bytes 67108864 | tf_op jit(solution)/shard_map/out_reduce/pallas_call | solution.py:465
  91.2 2.3 %write.1 = (bf16[128,16384]{1,0:T(8,128)(2,1)}, bf16[128,8,128]{2,1,0:T(8,128)(2,1)}, bf16[128,8,128]{2,1,0:T(8,128)(2,1)}) custom-call(bf16[128,16384]{1,0:T(8,128)(2,1)S(1)} %get-tuple-element.12.y_ref, bf16[128,8,128]{2,1,0:T(8,128)(2,1)S(1)} %get-tuple-element.13.k_ref, bf16[128,8,128]{2,1,0:T(8,128)(2,1)S(1)} %get-tuple-element.14.v_ref), custom_call_target="tpu_custom_call" | custom-call | tf_op jit(solution)/shard_map/write/pallas_call | solution.py:509

commit v6 on v5

--- a/solution.py
+++ b/solution.py
@@ -10,10 +10,12 @@
 MESH = pl.DeviceIdType.MESH
 CORES = 2
 ROUNDS = 8
+FIRST = 2
 WRITES = 8
-DEPTH = 512
+DEPTH = 1024
 SHORT = 32
-SHORT_STEP = 4
+SHORT_STEP = 8
+PITCH = 24
 PACK = 16
 LONG_STEP = 10
 OFFSETS = (2, 1, 3, 0)
@@ -27,8 +29,10 @@
     me = lax.axis_index("model")
     steps, rows, depth = xbuf.shape
     slots = wbuf.shape[0]
-    dim = qbuf.shape[1]
-    heads = qbuf.shape[0] // rows
+    dim = qbuf.shape[2]
+    heads = o_ref.shape[1] // dim
+    qflat, oflat = (ref.reshape(rows * PITCH, dim) for ref in (qbuf, obuf))
+    lines = pl.ds(0, heads)
     width = heads * dim
     context = klong.shape[1]
     unit = context // SHORT
@@ -112,7 +116,7 @@
     kv_ref[...] = kv
     kvf[...] = kv.astype(F32)
     for h in range(heads):
-        qbuf[pl.ds(h, rows, stride=heads), :] = acc[:, h * dim:(h + 1) * dim]
+        qflat[pl.ds(h, rows, stride=PITCH), :] = acc[:, h * dim:(h + 1) * dim]
 
     inv_sqrt = dim ** -0.5
     contract_last = (((1,), (1,)), ((), ()))
@@ -155,22 +159,34 @@
     place = jnp.where(own, jnp.where(col % SHORT == SHORT - 1, -1, col % SHORT), context)
     line = iota((1, context), 1)
 
-    @pl.loop(0, rows // unit // SHORT_STEP)
-    def _(group):
-        items, places = [], []
+    def short_items(group):
+        items = []
         for i in range(SHORT_STEP):
             first = (group * SHORT_STEP + i) * unit
             bound = jnp.zeros((1, context), jnp.int32)
             for j in range(unit):
                 bound = jnp.where(line // SHORT == j, lens[first + j], bound)
             seqs = pl.ds(pl.multiple_of(first, unit), unit)
-            lines = pl.ds(pl.multiple_of(first * heads, short_rows), short_rows)
-            places.append(lines)
             items.append((
-                qbuf[lines].astype(BF16),
+                seqs, qbuf[seqs, lines].reshape(short_rows, dim).astype(BF16),
                 kshort[seqs].reshape(context, dim), vshort[seqs].reshape(context, dim), place < bound))
-        for lines, out in zip(places, attend(items)):
-            obuf[lines] = out
+        return items
+
+    long_col = iota((heads, context), 1)
+    long_place = jnp.where(long_col == context - 1, -1, long_col)
+
+    def long_items(i):
+        items = []
+        for j in range(LONG_STEP):
+            slot = jnp.minimum(i * LONG_STEP + j, count - 1)
+            b = order[slot]
+            items.append((b, qbuf[b, lines].astype(BF16), klong[slot], vlong[slot], long_place < lens[b]))
+        return items
+
+    def work(items):
+        for item, out in zip(items, attend([item[1:] for item in items])):
+            here = obuf.at[item[0], lines]
+            here[...] = out.reshape(here.shape)
 
     @pl.loop(0, count)
     def _(i):
@@ -181,21 +197,20 @@
     def _(i):
         put_new(klong, vlong, i, context, order[i])
 
-    long_col = iota((heads, context), 1)
-    long_place = jnp.where(long_col == context - 1, -1, long_col)
-
-    @pl.loop(0, (count + LONG_STEP - 1) // LONG_STEP)
+    last = rows // unit // SHORT_STEP - 1
+
+    @pl.loop(0, last)
+    def _(group):
+        work(short_items(group))
+
+    work(short_items(last) + long_items(0))
+
+    @pl.loop(1, (count + LONG_STEP - 1) // LONG_STEP)
     def _(i):
-        slots = [jnp.minimum(i * LONG_STEP + j, count - 1) for j in range(LONG_STEP)]
-        seqs = [order[slot] for slot in slots]
-        lines = [pl.ds(pl.multiple_of(b * heads, heads), heads) for b in seqs]
-        outs = attend([(qbuf[here].astype(BF16), klong[slot], vlong[slot], long_place < lens[b])
-                       for here, slot, b in zip(lines, slots, seqs)])
-        for here, out in zip(lines, outs):
-            obuf[here] = out
+        work(long_items(i))
 
     for h in range(heads):
-        o_ref[:, h * dim:(h + 1) * dim] = obuf[pl.ds(h, rows, stride=heads), :].astype(BF16)
+        o_ref[:, h * dim:(h + 1) * dim] = oflat[pl.ds(h, rows, stride=PITCH), :].astype(BF16)
     pltpu.make_async_copy(first_ref, first_ref, first_sem).wait()
 
 
@@ -207,7 +222,7 @@
     steps = model // DEPTH
     sem = pltpu.SemaphoreType.DMA
     total = width + 2 * dim
-    first = pltpu.VMEM((len(OFFSETS), width, model // (ROUNDS * size) * CORES), BF16)
+    first = pltpu.VMEM((FIRST, width, model // (ROUNDS * size) * CORES), BF16)
     return pl.pallas_call(
         functools.partial(front_kernel, size),
         out_shape=(pltpu.VMEM((rows, width), BF16), pltpu.VMEM((rows, 2 * dim), BF16), first),
@@ -215,18 +230,18 @@
         out_specs=(pl.BlockSpec(memory_space=pltpu.VMEM),) * 3,
         scratch_shapes=[
             pltpu.VMEM((steps, rows, DEPTH), BF16),
-            pltpu.VMEM((4, DEPTH, total), BF16),
+            pltpu.VMEM((3, DEPTH, total), BF16),
             pltpu.VMEM((rows, total), F32),
             pltpu.VMEM((rows, 2 * dim), F32),
-            pltpu.VMEM((rows * heads, dim), F32),
-            pltpu.VMEM((rows * heads, dim), F32),
+            pltpu.VMEM((rows, PITCH, dim), F32),
+            pltpu.VMEM((rows, PITCH, dim), F32),
             pltpu.VMEM((rows, SHORT, dim), BF16),
             pltpu.VMEM((rows, SHORT, dim), BF16),
             pltpu.VMEM((rows, context, dim), BF16),
             pltpu.VMEM((rows, context, dim), BF16),
             pltpu.SMEM((rows,), jnp.int32),
             pltpu.SMEM((rows,), jnp.int32),
-            sem((4,)), sem((4,)), sem((2,)), sem((2,)), sem, sem,
+            sem((3,)), sem((3,)), sem((2,)), sem((2,)), sem, sem,
         ],
         compiler_params=pltpu.CompilerParams(vmem_limit_bytes=48 * 1024 * 1024),
         cost_estimate=pl.CostEstimate(
@@ -328,7 +343,7 @@
         forward(r, plus2, everything)
 
     for slot in range(slots):
-        slab(slots + slot, OFFSETS[0], slot).start()
+        slab(FIRST + slot, OFFSETS[0], slot).start()
     own_kv = pltpu.make_async_copy(kv_ref, kvs_ref.at[:, pl.ds(pl.multiple_of(me * nk, nk), nk)], kv_sem)
     own_kv.start()
 
@@ -367,20 +382,25 @@
             part[r, j, q] = product[:, q * n:(q + 1) * n]
         pair_copy(r, j).start()
 
-    @pl.loop(0, slots)
+    @pl.loop(0, FIRST)
     def _(r):
         multiply(r, 0, first_ref.at[r])
 
-        @pl.when(r >= 2)
-        def _():
-            send_hops(r - 2)
-
-    @pl.loop(slots, ROUNDS)
-    def _(r):
-        slot = r - slots
+    @pl.loop(FIRST, ROUNDS)
+    def _(r):
+        slot = lax.rem(r - FIRST, slots)
         slab(r, OFFSETS[0], slot).wait()
         multiply(r, 0, wbuf.at[slot])
-        slab(slot // 2, OFFSETS[1] + 2 * lax.rem(slot, 2), slot).start()
+
+        @pl.when(r < ROUNDS - slots)
+        def _():
+            slab(r + slots, OFFSETS[0], slot).start()
+
+        @pl.when(r >= ROUNDS - slots)
+        def _():
+            ahead = r - (ROUNDS - slots)
+            slab(ahead // 2, OFFSETS[1] + 2 * lax.rem(ahead, 2), slot).start()
+
         send_hops(r - 2)
 
     relay(None)
@@ -388,7 +408,7 @@
     @pl.loop(0, ROUNDS)
     def _(r):
         for way in range(2):
-            slot = 2 * lax.rem(r, 2) + way
+            slot = lax.rem(2 * r + way + ROUNDS - FIRST, slots)
             slab(r, OFFSETS[1 + way], slot).wait()
             multiply(r, 1 + way, wbuf.at[slot])
 
@@ -412,7 +432,7 @@
 
     @pl.loop(0, ROUNDS)
     def _(r):
-        slot = lax.rem(r, slots)
+        slot = lax.rem(r + 3 * ROUNDS - FIRST, slots)
         slab(r, OFFSETS[3], slot).wait()
         multiply(r, 3, wbuf.at[slot])
 

time: 93.5 us -> 91.5 us (0.979)
  Pallas kernels: 92.8 us -> 90.7 us
    pallas_call x1, Pallas kernels: 29.8 us -> 27.7 us  [front(): pl.pallas_call(functools.partial(front_kernel, size), out_shape=(pltpu.VM...]
where the time goes in v6:
time: 91.5 us; the launch traced here: 91.4 us
  Pallas kernels  90.7 us (99%)
    pallas_call x1, Pallas kernels, out_product(): pl.pallas_call(functools.partial(out_kernel, size), out_shape=(pltpu.VMEM...  60.8 us
    pallas_call x1, Pallas kernels, front(): pl.pallas_call(functools.partial(front_kernel, size), out_shape=(pltpu.VM...  27.7 us
    pallas_call x1, Pallas kernels, write(): pl.pallas_call(write_kernel, out_shape=tuple((jax.ShapeDtypeStruct(a.shap...  2.25 us

profile of v6, /device:TPU:113, one launch (start us, length us, event | category | flops | bytes accessed | tf_op | source)
XLA Modules:
  0.0 91.4 jit_solution(16329838906305198044)
XLA Ops:
  0.6 27.7 %front.1 = (bf16[128,2048]{1,0:T(8,128)(2,1)S(1)}, bf16[128,256]{1,0:T(8,128)(2,1)S(1)}, bf16[2,2048,512]{2,1,0:T(8,128)(2,1)S(1)}) custom-call(bf16[128,16384]{1,0:T(8,128)(2,1)} %x_ref.3, bf16[16384,2048]{1,0:T(8,128)(2,1)} %wq_ref.1, bf16[16384,1024]{1,0:T(8,128)(2,1)} %wk_ref.1, bf16[16384,1024]{1,0:T(8,128)(2,1)} %wv_ref.1, ...), custom_call_target="tpu_custom_call" | custom-call | flops 9663676416 | bytes 75497472 | tf_op jit(solution)/shard_map/front/pallas_call | solution.py:226
  28.3 60.8 %out_reduce.1 = (bf16[128,16384]{1,0:T(8,128)(2,1)S(1)}, bf16[128,8,128]{2,1,0:T(8,128)(2,1)S(1)}, bf16[128,8,128]{2,1,0:T(8,128)(2,1)S(1)}) custom-call(bf16[128,2048]{1,0:T(8,128)(2,1)S(1)} %get-tuple-element.9.o_ref, bf16[128,256]{1,0:T(8,128)(2,1)S(1)} %get-tuple-element.10.kv_ref, bf16[2,2048,512]{2,1,0:T(8,128)(2,1)S(1)} %get-tuple-element.11.first_ref, ...), custom_call_target="tpu_custom_call" | custom-call | flops 8589934592 | bytes 67108864 | tf_op jit(solution)/shard_map/out_reduce/pallas_call | solution.py:485
  89.1 2.3 %write.1 = (bf16[128,16384]{1,0:T(8,128)(2,1)}, bf16[128,8,128]{2,1,0:T(8,128)(2,1)}, bf16[128,8,128]{2,1,0:T(8,128)(2,1)}) custom-call(bf16[128,16384]{1,0:T(8,128)(2,1)S(1)} %get-tuple-element.12.y_ref, bf16[128,8,128]{2,1,0:T(8,128)(2,1)S(1)} %get-tuple-element.13.k_ref, bf16[128,8,128]{2,1,0:T(8,128)(2,1)S(1)} %get-tuple-element.14.v_ref), custom_call_target="tpu_custom_call" | custom-call | tf_op jit(solution)/shard_map/write/pallas_call | solution.py:529

commit v7 on v6

--- a/solution.py
+++ b/solution.py
@@ -11,7 +11,7 @@
 CORES = 2
 ROUNDS = 8
 FIRST = 2
-WRITES = 8
+WRITES = 2
 DEPTH = 1024
 SHORT = 32
 SHORT_STEP = 8
@@ -148,11 +148,6 @@
     for copy in short_copies():
         copy.wait()
 
-    @pl.loop(0, rows // unit)
-    def _(u):
-        for j in range(unit):
-            put_new(kshort, vshort, u * unit + j, SHORT, u * unit + j)
-
     short_rows = unit * heads
     col = iota((short_rows, context), 1)
     own = col // SHORT == iota((short_rows, 1), 0) // heads
@@ -160,6 +155,8 @@
     line = iota((1, context), 1)
 
     def short_items(group):
+        for i in range(SHORT_STEP * unit):
+            put_new(kshort, vshort, group * SHORT_STEP * unit + i, SHORT, group * SHORT_STEP * unit + i)
         items = []
         for i in range(SHORT_STEP):
             first = (group * SHORT_STEP + i) * unit
@@ -288,7 +285,7 @@
     PAIR, HOP, NEAR, GATHER, FORWARD = range(5)
 
     def pair_copy(r, j):
-        recv = pair_recv.at[(len(OFFSETS) - 1) * ROUNDS if j == len(OFFSETS) - 1 else j * ROUNDS + r]
+        recv = pair_recv.at[(0 * ROUNDS + r, ROUNDS + r, ROUNDS + r, 2 * ROUNDS)[j]]
         return remote(part.at[r, j, 1 - core], pair.at[r, j], sent.at[PAIR], recv, mate)
 
     def hop_copy(r, way):
@@ -360,7 +357,10 @@
     gather(None)
 
     def pair_sum(r, j):
-        pair_copy(r, j).wait_recv()
+        if j == 0:
+            pair_copy(r, j).wait_recv()
+        elif j == 1:
+            wait_for(pair.at[r, pl.ds(1, 2)], pair_recv.at[ROUNDS + r])
         part[r, j, core] = part[r, j, core] + pair[r, j]
 
     def send_hops(r):
@@ -452,7 +452,7 @@
             kv_heads[pl.ds(owner, rows, stride=size), :] = kvs_ref[:, owner * nk + i * dim:owner * nk + (i + 1) * dim].astype(F32)
         ref[...] = kv_heads[...].astype(BF16).reshape(ref.shape)
 
-    wait_for(pair.at[:, 3], pair_recv.at[3 * ROUNDS])
+    wait_for(pair.at[:, 3], pair_recv.at[2 * ROUNDS])
     pltpu.make_async_copy(xbuf, xbuf, x_sem).wait()
 
     @pl.loop(0, ROUNDS)
@@ -503,7 +503,7 @@
             pltpu.VMEM((ROUNDS, 2, rows // 2, n), F32),
             pltpu.VMEM((ROUNDS, 2, rows, n), F32),
             sem((4,)), sem, sem, sem((7,)),
-            sem((3 * ROUNDS + 1,)), sem((ROUNDS,)), sem((ROUNDS,)), sem((ROUNDS + 1,)), sem((ROUNDS + 1,)), sem((2,)),
+            sem((2 * ROUNDS + 1,)), sem((ROUNDS,)), sem((ROUNDS,)), sem((ROUNDS + 1,)), sem((ROUNDS + 1,)), sem((2,)),
         ],
         compiler_params=pltpu.CompilerParams(
             collective_id=0, has_side_effects=True, vmem_limit_bytes=36 * 1024 * 1024),

time: 91.5 us -> 91.3 us (level)
  no operation moved by 1% of the time
where the time goes in v7:
time: 91.3 us; the launch traced here: 90.6 us
  Pallas kernels  90 us (99%)
    pallas_call x1, Pallas kernels, out_product(): pl.pallas_call(functools.partial(out_kernel, size), out_shape=(pltpu.VMEM...  60.7 us
    pallas_call x1, Pallas kernels, front(): pl.pallas_call(functools.partial(front_kernel, size), out_shape=(pltpu.VM...  27.1 us
    pallas_call x1, Pallas kernels, write(): pl.pallas_call(write_kernel, out_shape=tuple((jax.ShapeDtypeStruct(a.shap...  2.2 us

profile of v7, /device:TPU:113, one launch (start us, length us, event | category | flops | bytes accessed | tf_op | source)
XLA Modules:
  0.0 90.6 jit_solution(2425183664022286872)
XLA Ops:
  0.6 27.1 %front.1 = (bf16[128,2048]{1,0:T(8,128)(2,1)S(1)}, bf16[128,256]{1,0:T(8,128)(2,1)S(1)}, bf16[2,2048,512]{2,1,0:T(8,128)(2,1)S(1)}) custom-call(bf16[128,16384]{1,0:T(8,128)(2,1)} %x_ref.3, bf16[16384,2048]{1,0:T(8,128)(2,1)} %wq_ref.1, bf16[16384,1024]{1,0:T(8,128)(2,1)} %wk_ref.1, bf16[16384,1024]{1,0:T(8,128)(2,1)} %wv_ref.1, ...), custom_call_target="tpu_custom_call" | custom-call | flops 9663676416 | bytes 75497472 | tf_op jit(solution)/shard_map/front/pallas_call | solution.py:223
  27.7 60.7 %out_reduce.1 = (bf16[128,16384]{1,0:T(8,128)(2,1)S(1)}, bf16[128,8,128]{2,1,0:T(8,128)(2,1)S(1)}, bf16[128,8,128]{2,1,0:T(8,128)(2,1)S(1)}) custom-call(bf16[128,2048]{1,0:T(8,128)(2,1)S(1)} %get-tuple-element.9.o_ref, bf16[128,256]{1,0:T(8,128)(2,1)S(1)} %get-tuple-element.10.kv_ref, bf16[2,2048,512]{2,1,0:T(8,128)(2,1)S(1)} %get-tuple-element.11.first_ref, ...), custom_call_target="tpu_custom_call" | custom-call | flops 8589934592 | bytes 67108864 | tf_op jit(solution)/shard_map/out_reduce/pallas_call | solution.py:485
  88.4 2.2 %write.1 = (bf16[128,16384]{1,0:T(8,128)(2,1)}, bf16[128,8,128]{2,1,0:T(8,128)(2,1)}, bf16[128,8,128]{2,1,0:T(8,128)(2,1)}) custom-call(bf16[128,16384]{1,0:T(8,128)(2,1)S(1)} %get-tuple-element.12.y_ref, bf16[128,8,128]{2,1,0:T(8,128)(2,1)S(1)} %get-tuple-element.13.k_ref, bf16[128,8,128]{2,1,0:T(8,128)(2,1)S(1)} %get-tuple-element.14.v_ref), custom_call_target="tpu_custom_call" | custom-call | tf_op jit(solution)/shard_map/write/pallas_call | solution.py:529
